TPU v7x, 128 devices: a whole 4x4x4 slice. The times are simulated.
128 devices in a mesh: dp: 1, tp: 2 (over core), cp: 64 (over z, y, x).
Axes of the slice: x: 4, y: 4, z: 4, core: 2. Of those that a mesh axis runs over, the one named last changes fastest.
Arguments:
- hidden: bfloat16 [2048, 3072], P(('dp', 'cp'))
- positions: int32 [2048], P(('dp', 'cp'))
- ln_gain: bfloat16 [3072], replicated
- w_q: bfloat16 [3072, 3072], P(None, 'tp')
- w_k: bfloat16 [3072, 1024], P(None, 'tp')
- w_v: bfloat16 [3072, 1024], P(None, 'tp')
- w_o: bfloat16 [3072, 3072], P('tp')
- w_gate: bfloat16 [3072, 8192], P(None, 'tp')
- w_up: bfloat16 [3072, 8192], P(None, 'tp')
- w_down: bfloat16 [8192, 3072], P('tp')
Outputs:
- output 1: bfloat16 [2048, 3072], P(('dp', 'cp'))
- output 2: bfloat16 [2048, 8, 128], P(('dp', 'cp'), 'tp')
- output 3: bfloat16 [2048, 8, 128], P(('dp', 'cp'), 'tp')
All inputs are finite; a program needn't handle non-finite values.
Results may differ from a plain program's by a relative error of at most 0.014011.
Values are sent between devices in bfloat16 or wider.
A program may use at most 1 GiB of HBM per device.

v0:
```python
import functools

import jax
import jax.numpy as jnp
import numpy as np
from jax import lax
from jax.experimental import pallas as pl
from jax.experimental.pallas import tpu as pltpu
from jax.sharding import PartitionSpec as P

HEAD_DIM = 128
ROPE_BASE = 4000000
LN_EPS = 1e-5
D = 3072
T = 32
R = 128
QW = 1536
KW = 512
GW = 384
FF = 1024
FFT = 4096
NO = 768
KC = 4
NEG = -1e30
F32 = jnp.float32
BF16 = jnp.bfloat16


def mm(a, b):
    return jnp.dot(a, b, preferred_element_type=F32)


def rope(x, cos, sin, even):
    left = pltpu.roll(x, 127, 1)
    right = pltpu.roll(x, 1, 1)
    return (x * cos + jnp.where(even, -left, right) * sin).astype(BF16)


def kernel(hid, pos, gain, invf, wq, wk, wv, wo, wg, wu, wd,
           out_h, out_k, out_v,
           wq_s, wk_s, wv_s, wo_s, wg_s, wu_s, wd_s,
           h_all, accq, acck, accv, q_my, q_all, kv_my, kv_all, s_s, o_my, o_cat,
           a_all, m_my, m_cat, m_oth, p_my, p_oth,
           w_sem, hs, hr, fs, fr, qs, qr, ks, kr, k1s, k1r, v1s, v1r, k2s, k2r, v2s, v2r,
           as_, ar, os_, orr, ms, mr, ds_, dr):
    tp = lax.axis_index('tp')
    cp = lax.axis_index('cp')
    x = lax.rem(cp, 4)
    y = lax.rem(cp // 4, 4)
    z = cp // 16

    def xp(d):
        return tp, z * 16 + y * 4 + lax.rem(x + d, 4)

    def yp(d):
        return tp, z * 16 + lax.rem(y + d, 4) * 4 + x

    def zp(d):
        return tp, lax.rem(z + d, 4) * 16 + y * 4 + x

    mate = (1 - tp, cp)

    def rcopy(src, dst, ss, rs, dev):
        return pltpu.make_async_remote_copy(
            src_ref=src, dst_ref=dst, send_sem=ss, recv_sem=rs,
            device_id={'tp': dev[0], 'cp': dev[1]}, device_id_type=pl.DeviceIdType.MESH)

    kc = D // KC
    wcp = []
    for i in range(KC):
        rows = pl.ds(i * kc, kc)
        for n, (src, dst) in enumerate(((wq, wq_s), (wk, wk_s), (wv, wv_s))):
            wcp.append(pltpu.make_async_copy(src.at[rows], dst.at[rows], w_sem.at[3 * i + n]))
    fcol = pl.ds(pl.multiple_of(x * FF, FF), FF)
    ncol = pl.ds(pl.multiple_of(x * NO, NO), NO)
    cg = pltpu.make_async_copy(wg.at[:, fcol], wg_s, w_sem.at[12])
    cu = pltpu.make_async_copy(wu.at[:, fcol], wu_s, w_sem.at[13])
    cd = pltpu.make_async_copy(wd.at[:, ncol], wd_s, w_sem.at[14])
    co = pltpu.make_async_copy(wo, wo_s, w_sem.at[15])
    for c in wcp + [cg, cu, cd, co]:
        c.start()

    barrier = pltpu.get_barrier_semaphore()
    peers = [f(d) for f in (xp, yp, zp) for d in (1, 2, 3)] + [mate]
    for dev in peers:
        pl.semaphore_signal(barrier, inc=1, device_id={'tp': dev[0], 'cp': dev[1]}, device_id_type=pl.DeviceIdType.MESH)

    hf = hid[...].astype(F32)
    mean = jnp.sum(hf, axis=-1, keepdims=True) * (1.0 / D)
    cen = hf - mean
    var = jnp.sum(cen * cen, axis=-1, keepdims=True) * (1.0 / D)
    h = (cen * lax.rsqrt(var + LN_EPS) * gain[...].astype(F32)).astype(BF16)
    myrows = pl.ds(pl.multiple_of(x * T, T), T)
    h_all[myrows, :] = h

    pl.semaphore_wait(barrier, len(peers))
    hcol = pl.ds(pl.multiple_of(tp * QW, QW), QW)
    hcp = []
    for d in (1, 3, 2):
        c = rcopy(h_all.at[myrows, hcol], h_all.at[myrows, hcol], hs.at[d - 1], hr.at[d - 1], xp(d))
        c.start()
        hcp.append((d, c))

    diag = lax.broadcasted_iota(jnp.int32, (T, T), 0) == lax.broadcasted_iota(jnp.int32, (T, T), 1)
    posf = jnp.sum(jnp.where(diag, jnp.broadcast_to(pos[...].astype(F32), (T, T)), 0.0), axis=1, keepdims=True)
    ang = posf * invf[...]
    cos = jnp.cos(ang)
    sin = jnp.sin(ang)
    even = lax.rem(lax.broadcasted_iota(jnp.int32, (T, HEAD_DIM), 1), 2) == 0

    for i in range(KC):
        rows = slice(i * kc, (i + 1) * kc)
        hi = h[:, rows]
        for n, (w, acc) in enumerate(((wq_s, accq), (wk_s, acck), (wv_s, accv))):
            wcp[3 * i + n].wait()
            part = mm(hi, w[rows, :])
            if i == 0:
                acc[...] = part
            else:
                acc[...] += part

    for j in range(4):
        cols = slice(j * HEAD_DIM, (j + 1) * HEAD_DIM)
        kj = rope(acck[:, cols].astype(BF16).astype(F32), cos, sin, even)
        vj = accv[:, cols].astype(BF16)
        kv_my[j, 0] = kj
        kv_my[j, 1] = vj
        out_k[:, cols] = kj
        out_v[:, cols] = vj
    kcp = []
    for d in (1, 2, 3):
        dst = lax.rem(x + d, 4)
        c = rcopy(kv_my.at[dst], kv_all.at[:, z, y, myrows], ks.at[d - 1], kr.at[d - 1], xp(d))
        c.start()
        kcp.append(c)
    kv_all[:, z, y, myrows, :] = kv_my[x]
    for j in range(12):
        cols = slice(j * HEAD_DIM, (j + 1) * HEAD_DIM)
        q_my[j // 3, :, (j % 3) * HEAD_DIM:(j % 3 + 1) * HEAD_DIM] = rope(
            accq[:, cols].astype(BF16).astype(F32), cos, sin, even)
    qcp = []
    for d in (1, 2, 3):
        dst = lax.rem(x + d, 4)
        c = rcopy(q_my.at[dst], q_all.at[myrows], qs.at[d - 1], qr.at[d - 1], xp(d))
        c.start()
        qcp.append(c)
    q_all[myrows, :] = q_my[x]

    fcp = []
    for d, c in hcp:
        c.wait_recv()
        frm = pl.ds(pl.multiple_of(lax.rem(x + 4 - d, 4) * T, T), T)
        f = rcopy(h_all.at[frm, hcol], h_all.at[frm, hcol], fs.at[d - 1], fr.at[d - 1], mate)
        f.start()
        fcp.append(f)

    for c in kcp:
        c.wait_recv()
    cps1 = []
    for d in (1, 3, 2):
        a = rcopy(kv_all.at[0, z, y], kv_all.at[0, z, y], k1s.at[d - 1], k1r.at[d - 1], yp(d))
        b = rcopy(kv_all.at[1, z, y], kv_all.at[1, z, y], v1s.at[d - 1], v1r.at[d - 1], zp(d))
        a.start()
        b.start()
        cps1 += [a, b]

    for f in fcp:
        f.wait_recv()

    def gate_up(i):
        cols = slice(i * 512, (i + 1) * 512)
        g = mm(h_all[...], wg_s[:, cols]).astype(BF16).astype(F32)
        u = mm(h_all[...], wu_s[:, cols]).astype(BF16).astype(F32)
        act = (g * jax.nn.sigmoid(g) * u).astype(BF16)
        a_all[x, :, cols] = act
        res = []
        for d in (1, 3, 2):
            c = rcopy(a_all.at[x, :, cols], a_all.at[x, :, cols],
                      as_.at[3 * i + d - 1], ar.at[3 * i + d - 1], xp(d))
            c.start()
            res.append(c)
        return res

    cg.wait()
    cu.wait()
    acp = gate_up(0)

    for c in cps1:
        c.wait_recv()
    cps2 = []
    for d in (1, 3, 2):
        a = rcopy(kv_all.at[0, z], kv_all.at[0, z], k2s.at[d - 1], k2r.at[d - 1], zp(d))
        b = rcopy(kv_all.at[1, :, y], kv_all.at[1, :, y], v2s.at[d - 1], v2r.at[d - 1], yp(d))
        a.start()
        b.start()
        cps2 += [a, b]

    acp += gate_up(1)

    for c in qcp:
        c.wait_recv()
    for c in cps2:
        c.wait_recv()

    q3 = jnp.concatenate([q_all[:, g * HEAD_DIM:(g + 1) * HEAD_DIM] for g in range(3)], axis=0)
    base = (z * 4 + y) * R
    row_tok = base + jnp.concatenate([lax.broadcasted_iota(jnp.int32, (R, 512), 0)] * 3, axis=0)
    col_tok = lax.broadcasted_iota(jnp.int32, (3 * R, 512), 1)

    def score_step(zz, row_max):
        kz = kv_all[0, zz].reshape(512, HEAD_DIM)
        s = lax.dot_general(q3, kz, (((1,), (1,)), ((), ())), preferred_element_type=F32) * (HEAD_DIM ** -0.5)
        s = jnp.where(col_tok + zz * 512 <= row_tok, s, NEG)
        s_s[zz] = s
        return jnp.maximum(row_max, jnp.max(s, axis=-1, keepdims=True))

    row_max = lax.fori_loop(0, z + 1, score_step, jnp.full((3 * R, 1), NEG, F32))

    def value_step(zz, state):
        row_sum, accum = state
        e = jnp.exp(s_s[zz] - row_max)
        vz = kv_all[1, zz].reshape(512, HEAD_DIM)
        return row_sum + jnp.sum(e, axis=-1, keepdims=True), accum + mm(e.astype(BF16), vz)

    row_sum, accum = lax.fori_loop(
        0, z + 1, value_step, (jnp.zeros((3 * R, 1), F32), jnp.zeros((3 * R, HEAD_DIM), F32)))
    o3 = (accum / row_sum).astype(BF16)
    for g in range(3):
        o_my[:, g * HEAD_DIM:(g + 1) * HEAD_DIM] = o3[g * R:(g + 1) * R]
    ocol = pl.ds(pl.multiple_of(x * GW, GW), GW)
    ocp = []
    for d in (1, 2, 3):
        rows = pl.ds(pl.multiple_of(lax.rem(x + d, 4) * T, T), T)
        c = rcopy(o_my.at[rows], o_cat.at[:, ocol], os_.at[d - 1], orr.at[d - 1], xp(d))
        c.start()
        ocp.append(c)
    o_cat[:, ocol] = o_my[myrows, :]

    for c in acp:
        c.wait_recv()
    cd.wait()
    macc = mm(a_all[0], wd_s[0:FF, :])
    for i in range(1, 4):
        macc = macc + mm(a_all[i], wd_s[i * FF:(i + 1) * FF, :])
    m_my[...] = macc.astype(BF16)
    mcp = []
    for d in (1, 2, 3):
        rows = pl.ds(pl.multiple_of(lax.rem(x + d, 4) * T, T), T)
        c = rcopy(m_my.at[rows], m_cat.at[:, ncol], ms.at[d - 1], mr.at[d - 1], xp(d))
        c.start()
        mcp.append(c)
    m_cat[:, ncol] = m_my[myrows, :]

    for c in ocp:
        c.wait_recv()
    co.wait()
    p_my[...] = mm(o_cat[...], wo_s[...]).astype(BF16)
    dp_ = rcopy(p_my, p_oth, ds_.at[0], dr.at[0], mate)
    dp_.start()
    for c in mcp:
        c.wait_recv()
    dm = rcopy(m_cat, m_oth, ds_.at[1], dr.at[1], mate)
    dm.start()
    dp_.wait_recv()
    attn = p_my[...].astype(F32) + p_oth[...].astype(F32)
    dm.wait_recv()
    out_h[...] = (hid[...].astype(F32) + attn + (m_cat[...].astype(F32) + m_oth[...].astype(F32))).astype(BF16)

    for c in [c for _, c in hcp] + fcp + qcp + kcp + cps1 + cps2 + acp + ocp + mcp + [dp_, dm]:
        c.wait_send()


def solution(mesh):
    inv = (1.0 / (np.float32(ROPE_BASE) ** (np.arange(0, HEAD_DIM, 2, dtype=np.float32) / np.float32(HEAD_DIM)))).astype(np.float32)
    inv = np.repeat(inv, 2).reshape(1, HEAD_DIM)

    def local_layer(hidden, positions, ln_gain, w_q, w_k, w_v, w_o, w_gate, w_up, w_down):
        vm = pl.BlockSpec(memory_space=pltpu.VMEM)
        hb = pl.BlockSpec(memory_space=pl.ANY)
        dma = pltpu.SemaphoreType.DMA
        V = pltpu.VMEM
        scratch = [
            V((D, QW), BF16), V((D, KW), BF16), V((D, KW), BF16), V((QW, D), BF16),
            V((D, FF), BF16), V((D, FF), BF16), V((FFT, NO), BF16),
            V((R, D), BF16), V((T, QW), F32), V((T, KW), F32), V((T, KW), F32),
            V((4, T, GW), BF16), V((R, GW), BF16), V((4, 2, T, HEAD_DIM), BF16),
            V((2, 4, 4, R, HEAD_DIM), BF16), V((4, 3 * R, 512), F32), V((R, GW), BF16), V((T, QW), BF16),
            V((4, R, FF), BF16), V((R, NO), BF16), V((T, D), BF16), V((T, D), BF16), V((T, D), BF16), V((T, D), BF16),
            dma((16,)), dma((3,)), dma((3,)), dma((3,)), dma((3,)), dma((3,)), dma((3,)), dma((3,)), dma((3,)),
            dma((3,)), dma((3,)), dma((3,)), dma((3,)), dma((3,)), dma((3,)), dma((3,)), dma((3,)),
            dma((6,)), dma((6,)), dma((3,)), dma((3,)), dma((3,)), dma((3,)), dma((2,)), dma((2,)),
        ]
        out_h, out_k, out_v = pl.pallas_call(
            kernel,
            name='layer',
            out_shape=(jax.ShapeDtypeStruct((T, D), BF16), jax.ShapeDtypeStruct((T, KW), BF16), jax.ShapeDtypeStruct((T, KW), BF16)),
            in_specs=[vm, vm, vm, vm] + [hb] * 7,
            out_specs=(vm, vm, vm),
            scratch_shapes=scratch,
            compiler_params=pltpu.CompilerParams(collective_id=0, has_side_effects=True, vmem_limit_bytes=67043328),
        )(hidden, positions.reshape(1, T), ln_gain.reshape(1, D), jnp.asarray(inv), w_q, w_k, w_v, w_o, w_gate, w_up, w_down)
        return out_h, out_k.reshape(T, 4, HEAD_DIM), out_v.reshape(T, 4, HEAD_DIM)

    row_spec = P(('dp', 'cp'), None)
    col_spec = P(None, 'tp')
    cache_spec = P(('dp', 'cp'), 'tp', None)
    in_specs = (row_spec, P(('dp', 'cp')), P(None), col_spec, col_spec, col_spec, P('tp', None), col_spec, col_spec, P('tp', None))
    return jax.shard_map(local_layer, mesh=mesh, in_specs=in_specs, out_specs=(row_spec, cache_spec, cache_spec), check_vma=False)
```

profile of v0, /device:TPU:1, one launch (start us, length us, event | category | flops | bytes accessed | tf_op | source)
XLA Modules:
  0.0 46.2 jit_solution(18372968206095095572)
XLA Ops:
  0.6 1.3 %reshape.19.gain = bf16[1,3072]{1,0:T(2,128)(2,1)} reshape(bf16[3072]{0:T(1024)(128)(2,1)} %param.13) | data formatting | bytes 12288 | tf_op jit(solution)/shard_map/reshape | solution.py:301
  1.9 39.9 %layer.1 = (bf16[32,3072]{1,0:T(8,128)(2,1)}, bf16[32,512]{1,0:T(8,128)(2,1)}, bf16[32,512]{1,0:T(8,128)(2,1)}) custom-call(bf16[32,3072]{1,0:T(8,128)(2,1)} %hid.1, s32[1,32]{1,0:T(1,128)} %bitcast.1, bf16[1,3072]{1,0:T(2,128)(2,1)} %reshape.19.gain, f32[1,128]{1,0:T(1,128)} %constant.2.clone.invf, bf16[3072,1536]{1,0:T(8,128)(2,1)} %wq.1, ...), custom_call_target="tpu_custom_call" | custom-call | tf_op jit(solution)/shard_map/layer/pallas_call | solution.py:293
  41.8 1.4 %reshape.20 = bf16[32,4,128]{2,1,0:T(4,128)(2,1)} reshape(bf16[32,512]{1,0:T(8,128)(2,1)} %get-tuple-element.7) | data formatting | bytes 65536 | tf_op jit(solution)/shard_map/reshape | solution.py:302
  43.2 1.4 %reshape.21 = bf16[32,4,128]{2,1,0:T(4,128)(2,1)} reshape(bf16[32,512]{1,0:T(8,128)(2,1)} %get-tuple-element.8) | data formatting | bytes 65536 | tf_op jit(solution)/shard_map/reshape | solution.py:302
  44.6 1.6 %copy.15 = bf16[32,3072]{1,0:T(8,128)(2,1)} copy(bf16[32,3072]{1,0:T(8,128)(2,1)} %get-tuple-element.12) | data formatting | bytes 393216
where the time goes:
time: 46.5 us; the launch traced here: 46.2 us
  Pallas kernels  39.9 us (86%)
  local copies, waits for them, and re-layouts  5.68 us (12%)
  between operations  0.64 us (1%)
    pallas_call x1, Pallas kernels, local_layer(): pl.pallas_call(kernel, name='layer', out_shape=(jax.ShapeDtypeStruct((T,...  39.9 us
    reshape x2, local copies, waits for them, and re-layouts, local_layer(): return (out_h, out_k.reshape(T, 4, HEAD_DIM), out_v.reshape(T, 4, HEAD_DIM))  2.77 us
    unnamed x1, local copies, waits for them, and re-layouts  1.62 us
    reshape x1, local copies, waits for them, and re-layouts, local_layer(): ln_gain.reshape(1, D)  1.3 us

commit v1 on v0

v1 whole, which is shorter than its diff:
```python
import jax
import jax.numpy as jnp
import numpy as np
from jax import lax
from jax.experimental import pallas as pl
from jax.experimental.pallas import tpu as pltpu
from jax.sharding import PartitionSpec as P

HEAD_DIM = 128
ROPE_BASE = 4000000
LN_EPS = 1e-5
D = 3072
T = 32
R = 128
QW = 1536
KW = 512
GW = 384
FF = 1024
FFT = 4096
KC = 4
NEG = -1e30
F32 = jnp.float32
BF16 = jnp.bfloat16
RING = (1, 3, 2)
KUP = (0, 1)
VUP = (1,)


def mm(a, b):
    return jnp.dot(a, b, preferred_element_type=F32)


def rope(x, cos, sin, even):
    left = pltpu.roll(x, 127, 1)
    right = pltpu.roll(x, 1, 1)
    return (x * cos + jnp.where(even, -left, right) * sin).astype(BF16)


def kernel(hid, pos, gain, invf, wq, wk, wv, wo, wg, wu, wd,
           out_h, out_k, out_v,
           hid_s, pos_s, gain_s, inv_s,
           wq_s, wk_s, wv_s, wo_s, wg_s, wu_s, wda_s, wdx_s,
           h_all, accq, acck, accv, kx, vx, q_my, q_all, kv_my, kv_all,
           mx_s, sum_s, acc_s, o_my, o_cat,
           a_my, a_cat, m_my, m_oth, p_my, p_oth,
           i_sem, w_sem, hs, hr, fs, fr, qs, qr, ks, kr, k1s, k1r, v1s, v1r, k2s, k2r, v2s, v2r,
           as_, ar, os_, orr, ds_, dr):
    scope = []

    def phase(name):
        if scope:
            scope.pop().__exit__(None, None, None)
        if name:
            scope.append(jax.named_scope(name))
            scope[0].__enter__()

    phase('start')
    tp = lax.axis_index('tp')
    cp = lax.axis_index('cp')
    x = lax.rem(cp, 4)
    y = lax.rem(cp // 4, 4)
    z = cp // 16

    def xp(d):
        return tp, z * 16 + y * 4 + lax.rem(x + d, 4)

    def yp(d):
        return tp, z * 16 + lax.rem(y + d, 4) * 4 + x

    def zp(d):
        return tp, lax.rem(z + d, 4) * 16 + y * 4 + x

    mate = (1 - tp, cp)

    def rcopy(src, dst, ss, rs, dev):
        return pltpu.make_async_remote_copy(
            src_ref=src, dst_ref=dst, send_sem=ss, recv_sem=rs,
            device_id={'tp': dev[0], 'cp': dev[1]}, device_id_type=pl.DeviceIdType.MESH)

    small = [pltpu.make_async_copy(a, b, i_sem.at[i])
             for i, (a, b) in enumerate(((hid, hid_s), (gain, gain_s), (pos, pos_s), (invf, inv_s)))]
    for c in small:
        c.start()
    kc = D // KC
    wcp = []
    for i in range(KC):
        rows = pl.ds(i * kc, kc)
        for n, (src, dst) in enumerate(((wq, wq_s), (wk, wk_s), (wv, wv_s))):
            wcp.append(pltpu.make_async_copy(src.at[rows], dst.at[rows], w_sem.at[3 * i + n]))
    fcol = pl.ds(pl.multiple_of(x * FF, FF), FF)
    cg = pltpu.make_async_copy(wg.at[:, fcol], wg_s, w_sem.at[12])
    cu = pltpu.make_async_copy(wu.at[:, fcol], wu_s, w_sem.at[13])
    cda = pltpu.make_async_copy(wd.at[pl.ds(0, FF)], wda_s, w_sem.at[14])
    low = pl.ds(FF, D)
    cdx = pltpu.make_async_copy(wd.at[low, pl.ds(QW + 2 * KW, KW)], wdx_s, w_sem.at[15])
    co = pltpu.make_async_copy(wo, wo_s, w_sem.at[16])
    cdq = pltpu.make_async_copy(wd.at[low, pl.ds(0, QW)], wq_s, w_sem.at[17])
    cdk = pltpu.make_async_copy(wd.at[low, pl.ds(QW, KW)], wk_s, w_sem.at[18])
    cdv = pltpu.make_async_copy(wd.at[low, pl.ds(QW + KW, KW)], wv_s, w_sem.at[19])
    for c in wcp[:3]:
        c.start()

    barrier = pltpu.get_barrier_semaphore()
    peers = [f(d) for f in (xp, yp, zp) for d in (1, 2, 3)] + [mate]
    for dev in peers:
        pl.semaphore_signal(barrier, inc=1, device_id={'tp': dev[0], 'cp': dev[1]}, device_id_type=pl.DeviceIdType.MESH)

    for yy in range(4):
        @pl.when(yy > y)
        def _(yy=yy):
            kv_all[1, z, yy] = jnp.zeros((R, HEAD_DIM), BF16)

        @pl.when(jnp.logical_and(yy > y, z == 3))
        def _(yy=yy):
            kv_all[0, z, yy] = jnp.zeros((R, HEAD_DIM), BF16)

    phase('ln')
    for c in small:
        c.wait()
    for c in wcp[3:] + [cg, cu, cda, cdx]:
        c.start()
    hf = hid_s[...].astype(F32)
    mean = jnp.sum(hf, axis=-1, keepdims=True) * (1.0 / D)
    cen = hf - mean
    var = jnp.sum(cen * cen, axis=-1, keepdims=True) * (1.0 / D)
    scaled = cen * lax.rsqrt(var + LN_EPS)
    gf = gain_s[...].astype(F32)
    myrows = pl.ds(pl.multiple_of(x * T, T), T)
    for i in range(D // HEAD_DIM):
        cols = slice(i * HEAD_DIM, (i + 1) * HEAD_DIM)
        h_all[myrows, cols] = (scaled[:, cols] * gf[i:i + 1]).astype(BF16)

    phase('tables')
    diag = lax.broadcasted_iota(jnp.int32, (T, T), 0) == lax.broadcasted_iota(jnp.int32, (T, T), 1)
    posf = jnp.sum(jnp.where(diag, jnp.broadcast_to(pos_s[...].astype(F32), (T, T)), 0.0), axis=1, keepdims=True)
    ang = posf * inv_s[...]
    cos = jnp.cos(ang)
    sin = jnp.sin(ang)
    even = lax.rem(lax.broadcasted_iota(jnp.int32, (T, HEAD_DIM), 1), 2) == 0

    def qkv(i):
        rows = slice(i * kc, (i + 1) * kc)
        hi = h_all[myrows, rows]
        for n, (w, acc) in enumerate(((wq_s, accq), (wk_s, acck), (wv_s, accv))):
            wcp[3 * i + n].wait()
            part = mm(hi, w[rows, :])
            if i == 0:
                acc[...] = part
            else:
                acc[...] += part

    hcol = pl.ds(pl.multiple_of(tp * QW, QW), QW)
    hhalf = [pl.ds(pl.multiple_of(tp * QW + n * (QW // 2), QW // 2), QW // 2) for n in range(2)]

    def hblock(frm, cols, n, dev, ss, rs):
        rows = pl.ds(pl.multiple_of(lax.rem(frm, 4) * T, T), T)
        b = h_all.at[rows, cols]
        return rcopy(b, b, ss.at[n], rs.at[n], dev)

    hcp = [hblock(x, hcol, 0, xp(1), hs, hr), hblock(x, hcol, 1, xp(3), hs, hr),
           hblock(x + 3, hhalf[0], 2, xp(1), hs, hr), hblock(x + 1, hhalf[1], 3, xp(3), hs, hr)]
    fcp = [hblock(x + 3, hcol, 0, mate, fs, fr), hblock(x + 1, hcol, 1, mate, fs, fr),
           hblock(x + 2, hhalf[0], 2, mate, fs, fr), hblock(x + 2, hhalf[1], 3, mate, fs, fr)]

    phase('qkv0')
    qkv(0)
    qkv(1)
    phase('barrier')
    pl.semaphore_wait(barrier, len(peers))
    hcp[0].start()
    hcp[1].start()
    phase('qkv1')
    qkv(2)
    qkv(3)
    for c in (cdq, cdk, cdv, co):
        c.start()

    phase('rope')
    for j in range(4):
        cols = slice(j * HEAD_DIM, (j + 1) * HEAD_DIM)
        kj = rope(acck[:, cols].astype(BF16).astype(F32), cos, sin, even)
        vj = accv[:, cols].astype(BF16)
        kv_my[j, 0] = kj
        kv_my[j, 1] = vj
        kx[pl.ds(j, T, stride=4), :] = kj.astype(F32)
        vx[pl.ds(j, T, stride=4), :] = vj.astype(F32)
    kcp = []
    for d in RING:
        dst = lax.rem(x + d, 4)
        c = rcopy(kv_my.at[dst], kv_all.at[:, z, y, myrows], ks.at[d - 1], kr.at[d - 1], xp(d))
        c.start()
        kcp.append(c)
    kv_all[:, z, y, myrows, :] = kv_my[x]
    for j in range(12):
        cols = slice(j * HEAD_DIM, (j + 1) * HEAD_DIM)
        q_my[j // 3, :, (j % 3) * HEAD_DIM:(j % 3 + 1) * HEAD_DIM] = rope(
            accq[:, cols].astype(BF16).astype(F32), cos, sin, even)
    qcp = []
    for d in RING:
        dst = lax.rem(x + d, 4)
        c = rcopy(q_my.at[dst], q_all.at[myrows], qs.at[d - 1], qr.at[d - 1], xp(d))
        c.start()
        qcp.append(c)
    q_all[myrows, :] = q_my[x]

    phase('hwait')
    for n in range(2):
        hcp[n].wait_recv()
        hcp[n + 2].start()
        fcp[n].start()

    def k1(d):
        b = kv_all.at[0, z, y]
        return rcopy(b, b, k1s.at[d - 1], k1r.at[d - 1], yp(d))

    def v1(d):
        b = kv_all.at[1, z, y]
        return rcopy(b, b, v1s.at[d - 1], v1r.at[d - 1], zp(d))

    def k2(dy, dz):
        row = {1: z, 3: z, 2: lax.rem(z + 3, 4) if dy in KUP else lax.rem(z + 1, 4)}[dz]
        b = kv_all.at[0, row, lax.rem(y + 4 - dy, 4)]
        dev = zp({1: 1, 3: 3, 2: 1 if dy in KUP else 3}[dz])
        return rcopy(b, b, k2s.at[3 * dy + dz - 1], k2r.at[3 * dy + dz - 1], dev)

    def v2(dz, dy):
        far = dy == 2 and dz > 0
        col = y if not far else lax.rem(y + (3 if dz in VUP else 1), 4)
        b = kv_all.at[1, lax.rem(z + 4 - dz, 4), col]
        dev = yp(dy if not far else (1 if dz in VUP else 3))
        return rcopy(b, b, v2s.at[3 * dz + dy - 1], v2r.at[3 * dz + dy - 1], dev)

    def k2_out(dy, dz):
        if dz == 1:
            return z <= 2
        if dz == 3:
            return z == 0 if dy in KUP else z <= 1
        return jnp.logical_or(z == 1, z == 2) if dy in KUP else jnp.logical_or(z == 3, z == 0)

    def k2_in(dy, dz):
        if dz == 1:
            return z >= 1
        if dz == 3:
            return z == 3 if dy in KUP else jnp.logical_or(z == 3, z == 0)
        return z >= 2

    k1_out = {d: jnp.logical_or(y + d <= 3, z < 3) for d in RING}
    k1_in = {d: jnp.logical_or(y >= d, z < 3) for d in RING}
    z_out = {d: z + d <= 3 for d in RING}
    z_in = {d: z >= d for d in RING}
    v20_out = {d: y + d <= 3 for d in RING}
    v20_in = {d: y >= d for d in RING}

    def when(cond, fn):
        pl.when(cond)(lambda: fn())

    phase('kvx')
    for c in kcp:
        c.wait_recv()
    for d in RING:
        when(k1_out[d], lambda d=d: k1(d).start())
        when(z_out[d], lambda d=d: v1(d).start())
    for d in RING:
        if d != 2:
            when(k2_out(0, d), lambda d=d: k2(0, d).start())
        when(v20_out[d], lambda d=d: v2(0, d).start())

    phase('hwait2')
    for n in (2, 3):
        hcp[n].wait_recv()
        fcp[n].start()
    for f in fcp:
        f.wait_recv()
    phase('guwait')
    cg.wait()
    cu.wait()

    def acopy(i, d):
        rows = pl.ds(pl.multiple_of(lax.rem(x + d, 4) * T, T), T)
        cols = pl.ds(pl.multiple_of(x * FF + i * 512, 512), 512)
        return rcopy(a_my.at[rows, pl.ds(i * 512, 512)], a_cat.at[:, cols],
                     as_.at[3 * i + d - 1], ar.at[3 * i + d - 1], xp(d))

    def gate_up(i):
        cols = slice(i * 512, (i + 1) * 512)
        g = mm(h_all[...], wg_s[:, cols]).astype(BF16).astype(F32)
        u = mm(h_all[...], wu_s[:, cols]).astype(BF16).astype(F32)
        a_my[:, cols] = (g * jax.nn.sigmoid(g) * u).astype(BF16)
        for d in RING:
            acopy(i, d).start()
        a_cat[:, pl.ds(pl.multiple_of(x * FF + i * 512, 512), 512)] = a_my[myrows, cols]

    phase('gu0')
    gate_up(0)

    phase('k1wait')
    for d in RING:
        when(k1_in[d], lambda d=d: k1(d).wait_recv())
        for dz in (1, 3):
            when(k2_out(d, dz), lambda d=d, dz=dz: k2(d, dz).start())

        @pl.when(z_in[d])
        def _(d=d):
            v1(d).wait_recv()
            for dy in (1, 3):
                v2(d, dy).start()

    phase('gu1')
    gate_up(1)

    phase('qwait')
    for c in qcp:
        c.wait_recv()
    q3 = jnp.concatenate([q_all[:, g * HEAD_DIM:(g + 1) * HEAD_DIM] for g in range(3)], axis=0)

    def scores(zz):
        kz = kv_all[0, zz].reshape(512, HEAD_DIM)
        return lax.dot_general(q3, kz, (((1,), (1,)), ((), ())), preferred_element_type=F32) * (HEAD_DIM ** -0.5)

    for d in RING:
        when(v20_in[d], lambda d=d: v2(0, d).wait_recv())
    phase('row0')
    row_tok = y * R + jnp.concatenate([lax.broadcasted_iota(jnp.int32, (R, 512), 0)] * 3, axis=0)
    col_tok = lax.broadcasted_iota(jnp.int32, (3 * R, 512), 1)
    s = jnp.where(col_tok <= row_tok, scores(z), NEG)
    m0 = jnp.max(s, axis=-1, keepdims=True)
    e = jnp.exp(s - m0)
    mx_s[...] = m0
    sum_s[...] = jnp.sum(e, axis=-1, keepdims=True)
    acc_s[...] = mm(e.astype(BF16), kv_all[1, z].reshape(512, HEAD_DIM))

    phase('relay')
    for i, dy in enumerate((0, 1, 3, 2)):
        for dz, up in ((1, True), (3, False)):
            when(k2_in(dy, dz), lambda dy=dy, dz=dz: k2(dy, dz).wait_recv())
            if (dy in KUP) == up:
                when(k2_out(dy, 2), lambda dy=dy: k2(dy, 2).start())
        if i:
            dz = dy

            @pl.when(z_in[dz])
            def _(dz=dz):
                for dd, up in ((1, True), (3, False)):
                    v2(dz, dd).wait_recv()
                    if (dz in VUP) == up:
                        v2(dz, 2).start()

    for dz in RING:
        phase(f'row{dz}')

        @pl.when(z_in[dz])
        def _(dz=dz):
            zz = z - dz
            if dz == 2:
                for dy in range(4):
                    k2(dy, 2).wait_recv()
            v2(dz, 2).wait_recv()
            s = scores(zz)
            m_old = mx_s[...]
            m_new = jnp.maximum(m_old, jnp.max(s, axis=-1, keepdims=True))
            e = jnp.exp(s - m_new)
            f = jnp.exp(m_old - m_new)
            mx_s[...] = m_new
            sum_s[...] = sum_s[...] * f + jnp.sum(e, axis=-1, keepdims=True)
            acc_s[...] = acc_s[...] * f + mm(e.astype(BF16), kv_all[1, zz].reshape(512, HEAD_DIM))

    phase('osend')
    o3 = (acc_s[...] / sum_s[...]).astype(BF16)
    for g in range(3):
        o_my[:, g * HEAD_DIM:(g + 1) * HEAD_DIM] = o3[g * R:(g + 1) * R]
    ocol = pl.ds(pl.multiple_of(x * GW, GW), GW)
    ocp = []
    for d in RING:
        rows = pl.ds(pl.multiple_of(lax.rem(x + d, 4) * T, T), T)
        c = rcopy(o_my.at[rows], o_cat.at[:, ocol], os_.at[d - 1], orr.at[d - 1], xp(d))
        c.start()
        ocp.append(c)
    o_cat[:, ocol] = o_my[myrows, :]
    out_k[...] = kx[...].astype(BF16)
    out_v[...] = vx[...].astype(BF16)

    phase('await')
    for i in range(2):
        for d in RING:
            acopy(i, d).wait_recv()
    phase('wdwait')
    for c in (cda, cdx, cdq, cdk, cdv):
        c.wait()
    phase('down')
    a_lo = a_cat[:, 0:FF]
    a_hi = a_cat[:, FF:]
    at = 0
    for w in (wq_s, wk_s, wv_s, wdx_s):
        n = w.shape[1]
        m_my[:, at:at + n] = (mm(a_hi, w[...]) + mm(a_lo, wda_s[:, at:at + n])).astype(BF16)
        at += n
    dm = rcopy(m_my, m_oth, ds_.at[1], dr.at[1], mate)
    dm.start()

    phase('owait')
    for c in ocp:
        c.wait_recv()
    co.wait()
    phase('wo')
    p_my[...] = mm(o_cat[...], wo_s[...]).astype(BF16)
    dp_ = rcopy(p_my, p_oth, ds_.at[0], dr.at[0], mate)
    dp_.start()
    phase('final')
    dm.wait_recv()
    rest = hid_s[...].astype(F32) + (m_my[...].astype(F32) + m_oth[...].astype(F32))
    dp_.wait_recv()
    out_h[...] = (rest + (p_my[...].astype(F32) + p_oth[...].astype(F32))).astype(BF16)

    phase('drain')
    for c in hcp + fcp + qcp + kcp + ocp + [dm, dp_]:
        c.wait_send()
    for i in range(2):
        for d in RING:
            acopy(i, d).wait_send()
    for d in RING:
        when(k1_out[d], lambda d=d: k1(d).wait_send())
        when(v20_out[d], lambda d=d: v2(0, d).wait_send())

        for dy in range(4):
            when(k2_out(dy, d), lambda d=d, dy=dy: k2(dy, d).wait_send())
        when(z_out[d], lambda d=d: v1(d).wait_send())

        @pl.when(z_in[d])
        def _(d=d):
            for dy in RING:
                v2(d, dy).wait_send()
    phase(None)


def emit(h, k, v, out_h, out_k, out_v, sem):
    cps = [pltpu.make_async_copy(a, b, sem.at[i]) for i, (a, b) in enumerate(((h, out_h), (k, out_k), (v, out_v)))]
    for c in cps:
        c.start()
    for c in cps:
        c.wait()


def solution(mesh):
    inv = (1.0 / (np.float32(ROPE_BASE) ** (np.arange(0, HEAD_DIM, 2, dtype=np.float32) / np.float32(HEAD_DIM)))).astype(np.float32)
    inv = np.repeat(inv, 2).reshape(1, HEAD_DIM)

    def local_layer(hidden, positions, ln_gain, w_q, w_k, w_v, w_o, w_gate, w_up, w_down):
        vm = pl.BlockSpec(memory_space=pltpu.VMEM)
        hb = pl.BlockSpec(memory_space=pl.ANY)
        dma = pltpu.SemaphoreType.DMA
        V = pltpu.VMEM
        scratch = [
            V((T, D), BF16), V((1, T), jnp.int32), V((D // HEAD_DIM, HEAD_DIM), BF16), V((1, HEAD_DIM), F32),
            V((D, QW), BF16), V((D, KW), BF16), V((D, KW), BF16), V((QW, D), BF16),
            V((D, FF), BF16), V((D, FF), BF16), V((FF, D), BF16), V((D, KW), BF16),
            V((R, D), BF16), V((T, QW), F32), V((T, KW), F32), V((T, KW), F32), V((R, HEAD_DIM), F32), V((R, HEAD_DIM), F32),
            V((4, T, GW), BF16), V((R, GW), BF16), V((4, 2, T, HEAD_DIM), BF16), V((2, 4, 4, R, HEAD_DIM), BF16),
            V((3 * R, 1), F32), V((3 * R, 1), F32), V((3 * R, HEAD_DIM), F32), V((R, GW), BF16), V((T, QW), BF16),
            V((R, FF), BF16), V((T, FFT), BF16), V((T, D), BF16), V((T, D), BF16), V((T, D), BF16), V((T, D), BF16),
            dma((4,)), dma((20,)), dma((4,)), dma((4,)), dma((4,)), dma((4,)), dma((3,)), dma((3,)), dma((3,)), dma((3,)),
            dma((3,)), dma((3,)), dma((3,)), dma((3,)), dma((12,)), dma((12,)), dma((12,)), dma((12,)),
            dma((6,)), dma((6,)), dma((3,)), dma((3,)), dma((2,)), dma((2,)),
        ]
        outs = (jax.ShapeDtypeStruct((T, D), BF16), jax.ShapeDtypeStruct((R, HEAD_DIM), BF16), jax.ShapeDtypeStruct((R, HEAD_DIM), BF16))
        res = pl.pallas_call(
            kernel,
            name='layer',
            out_shape=tuple(pltpu.VMEM(o.shape, o.dtype) for o in outs),
            in_specs=[hb] * 11,
            out_specs=(vm, vm, vm),
            scratch_shapes=scratch,
            compiler_params=pltpu.CompilerParams(collective_id=0, has_side_effects=True, vmem_limit_bytes=60000000),
        )(hidden, positions.reshape(1, T), ln_gain.reshape(D // HEAD_DIM, HEAD_DIM), jnp.asarray(inv),
          w_q, w_k, w_v, w_o, w_gate, w_up, w_down)
        out_h, out_k, out_v = pl.pallas_call(
            emit,
            name='emit',
            out_shape=outs,
            in_specs=[vm] * 3,
            out_specs=(hb, hb, hb),
            scratch_shapes=[dma((3,))],
        )(*[pltpu.with_memory_space_constraint(r, pltpu.VMEM) for r in res])
        return out_h, out_k.reshape(T, 4, HEAD_DIM), out_v.reshape(T, 4, HEAD_DIM)

    row_spec = P(('dp', 'cp'), None)
    col_spec = P(None, 'tp')
    cache_spec = P(('dp', 'cp'), 'tp', None)
    in_specs = (row_spec, P(('dp', 'cp')), P(None), col_spec, col_spec, col_spec, P('tp', None), col_spec, col_spec, P('tp', None))
    return jax.shard_map(local_layer, mesh=mesh, in_specs=in_specs, out_specs=(row_spec, cache_spec, cache_spec), check_vma=False)
```

time: 46.5 us -> 35.9 us (0.77)
  the two profiles are of different devices: /device:TPU:1 before, /device:TPU:97 now
where the time goes in v1:
time: 35.9 us; the launch traced here: 35.8 us
  Pallas kernels  35.2 us (98%)
  between operations  0.64 us (2%)
    pallas_call x1, Pallas kernels, local_layer(): pl.pallas_call(kernel, name='layer', out_shape=tuple((pltpu.VMEM(o.shape,...  34.5 us
    pallas_call x1, Pallas kernels, local_layer(): pl.pallas_call(emit, name='emit', out_shape=outs, in_specs=[vm] * 3, out_...  0.72 us

profile of v1, /device:TPU:97, one launch (start us, length us, event | category | flops | bytes accessed | tf_op | source)
XLA Modules:
  0.0 35.8 jit_solution(968490021539993723)
XLA Ops:
  0.6 34.5 %layer.1 = (bf16[32,3072]{1,0:T(8,128)(2,1)S(1)}, bf16[128,128]{1,0:T(8,128)(2,1)S(1)}, bf16[128,128]{1,0:T(8,128)(2,1)S(1)}) custom-call(bf16[32,3072]{1,0:T(8,128)(2,1)} %hid.1, s32[1,32]{1,0:T(1,128)} %bitcast.5, bf16[24,128]{1,0:T(8,128)(2,1)} %bitcast.4, f32[1,128]{1,0:T(1,128)} %constant.2.clone.invf, bf16[3072,1536]{1,0:T(8,128)(2,1)} %wq.1, ...), custom_call_target="tpu_custom_call" | custom-call | tf_op jit(solution)/shard_map/layer/pallas_call | solution.py:465
  35.1 0.7 %emit.1 = (bf16[32,3072]{1,0:T(8,128)(2,1)}, bf16[128,128]{1,0:T(8,128)(2,1)}, bf16[128,128]{1,0:T(8,128)(2,1)}) custom-call(bf16[32,3072]{1,0:T(8,128)(2,1)S(1)} %get-tuple-element.9.h, bf16[128,128]{1,0:T(8,128)(2,1)S(1)} %get-tuple-element.10.k, bf16[128,128]{1,0:T(8,128)(2,1)S(1)} %get-tuple-element.11.v), custom_call_target="tpu_custom_call" | custom-call | tf_op jit(solution)/shard_map/emit/pallas_call | solution.py:475

commit v2 on v1

v2 whole, which is shorter than its diff:
```python
import jax
import jax.numpy as jnp
import numpy as np
from jax import lax
from jax.experimental import pallas as pl
from jax.experimental.pallas import tpu as pltpu
from jax.sharding import PartitionSpec as P

HEAD_DIM = 128
ROPE_BASE = 4000000
LN_EPS = 1e-5
D = 3072
T = 32
R = 128
QW = 1536
KW = 512
GW = 384
T2 = 64
FF = 2048
FC = 1024
LO = 1024
FFT = 4096
KC = 4
NG = 512
NEG = -1e30
F32 = jnp.float32
BF16 = jnp.bfloat16
RING = (1, 3, 2)


def mm(a, b):
    return jnp.dot(a, b, preferred_element_type=F32)


def rope(x, cos, sin, even):
    left = pltpu.roll(x, 127, 1)
    right = pltpu.roll(x, 1, 1)
    return (x * cos + jnp.where(even, -left, right) * sin).astype(BF16)


def kernel(hid, pos, gain, invf, wq, wk, wv, wo, wg, wu, wd,
           out_h, out_k, out_v,
           hid_s, pos_s, gain_s, inv_s,
           wq_s, wk_s, wv_s, wg_s, wu_s, wda_s, wdx_s,
           h_all, accq, acck, accv, kx, vx, q_my, q_all, kv_my, kv_all,
           mx_s, sum_s, acc_s, o_my, o_cat,
           a_my, a_cat, m_my, m_oth, p_my, p_oth,
           i_sem, w_sem, hs, hr, fs, fr, qs, qr, ks, kr, k1s, k1r, v1s, v1r, k2s, k2r, v2s, v2r,
           as_, ar, os_, orr, ds_, dr):
    scope = []

    def phase(name):
        if scope:
            scope.pop().__exit__(None, None, None)
        if name:
            scope.append(jax.named_scope(name))
            scope[0].__enter__()

    phase('start')
    tp = lax.axis_index('tp')
    cp = lax.axis_index('cp')
    x = lax.rem(cp, 4)
    y = lax.rem(cp // 4, 4)
    z = cp // 16

    def xp(d):
        return tp, z * 16 + y * 4 + lax.rem(x + d, 4)

    def yp(d):
        return tp, z * 16 + lax.rem(y + d, 4) * 4 + x

    def zp(d):
        return tp, lax.rem(z + d, 4) * 16 + y * 4 + x

    mate = (1 - tp, cp)

    def rcopy(src, dst, ss, rs, dev):
        return pltpu.make_async_remote_copy(
            src_ref=src, dst_ref=dst, send_sem=ss, recv_sem=rs,
            device_id={'tp': dev[0], 'cp': dev[1]}, device_id_type=pl.DeviceIdType.MESH)

    small = [pltpu.make_async_copy(a, b, i_sem.at[i])
             for i, (a, b) in enumerate(((hid, hid_s), (gain, gain_s), (pos, pos_s), (invf, inv_s)))]
    for c in small:
        c.start()
    half = D // 2
    ckv = [pltpu.make_async_copy(src.at[pl.ds(i * half, half)], dst.at[pl.ds(i * half, half)], w_sem.at[2 * i + n])
           for i in range(2) for n, (src, dst) in enumerate(((wk, wk_s), (wv, wv_s)))]
    kc = D // KC
    cwq = [pltpu.make_async_copy(wq.at[pl.ds(i * kc, kc)], wq_s.at[pl.ds(i * kc, kc)], w_sem.at[4 + i]) for i in range(KC)]
    par = lax.rem(x, 2)
    pair = (tp, cp + 1 - 2 * par)
    mine = pl.ds(pl.multiple_of(par * T, T), T)
    theirs = pl.ds(pl.multiple_of((1 - par) * T, T), T)
    hcol = pl.ds(pl.multiple_of(tp * QW, QW), QW)
    cgu = [pltpu.make_async_copy(src.at[:, pl.ds(pl.multiple_of(par * FF + i * FC, FC), FC)],
                                 dst.at[:, pl.ds(i * FC, FC)], w_sem.at[8 + 2 * i + n])
           for i in range(2) for n, (src, dst) in enumerate(((wg, wg_s), (wu, wu_s)))]
    cda = pltpu.make_async_copy(wd.at[pl.ds(0, LO)], wda_s, w_sem.at[16])
    woref = [wg_s.at[pl.ds(0, QW), pl.ds(0, 1024)], wg_s.at[pl.ds(0, QW), pl.ds(1024, 1024)], wg_s.at[pl.ds(QW, QW), pl.ds(0, 1024)]]
    co = [pltpu.make_async_copy(wo.at[:, pl.ds(i * 1024, 1024)], woref[i], w_sem.at[17 + i]) for i in range(3)]
    groups = [(wdx_s.at[:], 5 * NG), (wk_s.at[:], 3 * NG), (wv_s.at[:], 4 * NG)] + [
        (wq_s.at[:, pl.ds(i * NG, NG)], i * NG) for i in range(3)]
    low = pl.ds(LO, D)
    cdw = [pltpu.make_async_copy(wd.at[low, pl.ds(at, NG)], ref, w_sem.at[20 + i]) for i, (ref, at) in enumerate(groups)]
    barrier = pltpu.get_barrier_semaphore()
    peers = [f(d) for f in (xp, yp, zp) for d in (1, 2, 3)] + [mate]
    for dev in peers:
        pl.semaphore_signal(barrier, inc=1, device_id={'tp': dev[0], 'cp': dev[1]}, device_id_type=pl.DeviceIdType.MESH)

    h_all[T2:R, :] = jnp.zeros((R - T2, D), BF16)
    a_cat[T:R, :] = jnp.zeros((R - T, FFT), BF16)
    o_cat[T:R, :] = jnp.zeros((R - T, QW), BF16)

    for yy in range(4):
        @pl.when(yy > y)
        def _(yy=yy):
            kv_all[1, z, yy] = jnp.zeros((R, HEAD_DIM), BF16)

        @pl.when(jnp.logical_and(yy > y, z == 3))
        def _(yy=yy):
            kv_all[0, z, yy] = jnp.zeros((R, HEAD_DIM), BF16)

    phase('ln')
    for c in small:
        c.wait()
    for c in ckv + cwq + cgu + [cda, cdw[0]]:
        c.start()
    hf = hid_s[...].astype(F32)
    mean = jnp.sum(hf, axis=-1, keepdims=True) * (1.0 / D)
    cen = hf - mean
    var = jnp.sum(cen * cen, axis=-1, keepdims=True) * (1.0 / D)
    scaled = cen * lax.rsqrt(var + LN_EPS)
    gf = gain_s[...].astype(F32)
    myrows = pl.ds(pl.multiple_of(x * T, T), T)
    for i in range(D // HEAD_DIM):
        cols = slice(i * HEAD_DIM, (i + 1) * HEAD_DIM)
        h_all[mine, cols] = (scaled[:, cols] * gf[i:i + 1]).astype(BF16)

    hcp = rcopy(h_all.at[mine, hcol], h_all.at[mine, hcol], hs.at[0], hr.at[0], pair)
    fcp = rcopy(h_all.at[theirs, hcol], h_all.at[theirs, hcol], fs.at[0], fr.at[0], mate)
    kcp = {d: rcopy(kv_my.at[lax.rem(x + d, 4)], kv_all.at[:, z, y, myrows], ks.at[d - 1], kr.at[d - 1], xp(d)) for d in RING}

    phase('tables')
    diag = lax.broadcasted_iota(jnp.int32, (T, T), 0) == lax.broadcasted_iota(jnp.int32, (T, T), 1)
    posf = jnp.sum(jnp.where(diag, jnp.broadcast_to(pos_s[...].astype(F32), (T, T)), 0.0), axis=1, keepdims=True)
    ang = posf * inv_s[...]
    cos = jnp.cos(ang)
    sin = jnp.sin(ang)
    even = lax.rem(lax.broadcasted_iota(jnp.int32, (T, HEAD_DIM), 1), 2) == 0

    phase('kvproj')
    for i in range(2):
        rows = slice(i * half, (i + 1) * half)
        for n, (w, acc) in enumerate(((wk_s, acck), (wv_s, accv))):
            ckv[2 * i + n].wait()
            part = mm(h_all[mine, rows], w[rows, :])
            if i == 0:
                acc[...] = part
            else:
                acc[...] += part
    phase('kvrope')
    for j in range(4):
        cols = slice(j * HEAD_DIM, (j + 1) * HEAD_DIM)
        kj = rope(acck[:, cols].astype(BF16).astype(F32), cos, sin, even)
        vj = accv[:, cols].astype(BF16)
        kv_my[j, 0] = kj
        kv_my[j, 1] = vj
        kx[pl.ds(j, T, stride=4), :] = kj.astype(F32)
        vx[pl.ds(j, T, stride=4), :] = vj.astype(F32)
    kv_all[:, z, y, myrows, :] = kv_my[x]

    phase('barrier')
    pl.semaphore_wait(barrier, len(peers))
    for d in RING:
        kcp[d].start()
    hcp.start()

    phase('qproj')
    for i in range(KC):
        rows = slice(i * kc, (i + 1) * kc)
        cwq[i].wait()
        part = mm(h_all[mine, rows], wq_s[rows, :])
        if i == 0:
            accq[...] = part
        else:
            accq[...] += part
    for c in cdw[1:]:
        c.start()

    def k1(d):
        b = kv_all.at[0, z, y]
        return rcopy(b, b, k1s.at[d - 1], k1r.at[d - 1], yp(d))

    def v1(d):
        b = kv_all.at[1, z, y]
        return rcopy(b, b, v1s.at[d - 1], v1r.at[d - 1], zp(d))

    def k2(dy, dz):
        b = kv_all.at[0, z, lax.rem(y + 4 - dy, 4)]
        return rcopy(b, b, k2s.at[3 * dy + dz - 1], k2r.at[3 * dy + dz - 1], zp(dz))

    def v2(dz, dy):
        b = kv_all.at[1, lax.rem(z + 4 - dz, 4), y]
        return rcopy(b, b, v2s.at[3 * dz + dy - 1], v2r.at[3 * dz + dy - 1], yp(dy))

    k1_out = {d: jnp.logical_or(y + d <= 3, z < 3) for d in RING}
    k1_in = {d: jnp.logical_or(y >= d, z < 3) for d in RING}
    z_out = {d: z + d <= 3 for d in RING}
    z_in = {d: z >= d for d in RING}
    v20_out = {d: y + d <= 3 for d in RING}
    v20_in = {d: y >= d for d in RING}

    def when(cond, fn):
        pl.when(cond)(lambda: fn())

    phase('kvx')
    for d in RING:
        kcp[d].wait_recv()
    for d in RING:
        when(k1_out[d], lambda d=d: k1(d).start())
        when(z_out[d], lambda d=d: v1(d).start())
    for d in RING:
        when(z_out[d], lambda d=d: k2(0, d).start())
    for d in RING:
        when(v20_out[d], lambda d=d: v2(0, d).start())

    phase('hwait')
    hcp.wait_recv()
    fcp.start()

    phase('qrope')
    for j in range(12):
        cols = slice(j * HEAD_DIM, (j + 1) * HEAD_DIM)
        q_my[j // 3, :, (j % 3) * HEAD_DIM:(j % 3 + 1) * HEAD_DIM] = rope(
            accq[:, cols].astype(BF16).astype(F32), cos, sin, even)
    qcp = []
    for d in RING:
        dst = lax.rem(x + d, 4)
        c = rcopy(q_my.at[dst], q_all.at[myrows], qs.at[d - 1], qr.at[d - 1], xp(d))
        c.start()
        qcp.append(c)
    q_all[myrows, :] = q_my[x]

    def acopy(i):
        cols = pl.ds(pl.multiple_of(par * FF + i * FC, FC), FC)
        return rcopy(a_my.at[theirs, pl.ds(i * FC, FC)], a_cat.at[pl.ds(0, T), cols], as_.at[i], ar.at[i], pair)

    phase('fwait')
    fcp.wait_recv()
    def gate_up(i):
        phase(f'gu{i}')
        cols = slice(i * FC, (i + 1) * FC)
        cgu[2 * i].wait()
        g = mm(h_all[...], wg_s[:, cols])[0:T2].astype(BF16).astype(F32)
        cgu[2 * i + 1].wait()
        u = mm(h_all[...], wu_s[:, cols])[0:T2].astype(BF16).astype(F32)
        a_my[:, cols] = (g * jax.nn.sigmoid(g) * u).astype(BF16)
        acopy(i).start()
        a_cat[0:T, pl.ds(pl.multiple_of(par * FF + i * FC, FC), FC)] = a_my[mine, cols]
    gate_up(0)
    phase('k1wait')
    for d in RING:
        when(k1_in[d], lambda d=d: k1(d).wait_recv())
        for dz in RING:
            when(z_out[dz], lambda d=d, dz=dz: k2(d, dz).start())

        @pl.when(z_in[d])
        def _(d=d):
            v1(d).wait_recv()
            for dy in RING:
                v2(d, dy).start()
    gate_up(1)
    for c in co:
        c.start()

    phase('qwait')
    for c in qcp:
        c.wait_recv()
    q3 = jnp.concatenate([q_all[:, g * HEAD_DIM:(g + 1) * HEAD_DIM] for g in range(3)], axis=0)

    def scores(zz):
        kz = kv_all[0, zz].reshape(512, HEAD_DIM)
        return lax.dot_general(q3, kz, (((1,), (1,)), ((), ())), preferred_element_type=F32) * (HEAD_DIM ** -0.5)

    for d in RING:
        when(v20_in[d], lambda d=d: v2(0, d).wait_recv())
    phase('row0')
    row_tok = y * R + jnp.concatenate([lax.broadcasted_iota(jnp.int32, (R, 512), 0)] * 3, axis=0)
    col_tok = lax.broadcasted_iota(jnp.int32, (3 * R, 512), 1)
    s = jnp.where(col_tok <= row_tok, scores(z), NEG)
    m0 = jnp.max(s, axis=-1, keepdims=True)
    e = jnp.exp(s - m0)
    mx_s[...] = m0
    sum_s[...] = jnp.sum(e, axis=-1, keepdims=True)
    acc_s[...] = mm(e.astype(BF16), kv_all[1, z].reshape(512, HEAD_DIM))

    for dz in RING:
        phase(f'row{dz}')

        @pl.when(z_in[dz])
        def _(dz=dz):
            zz = z - dz
            for dy in (0,) + RING:
                k2(dy, dz).wait_recv()
            for dy in RING:
                v2(dz, dy).wait_recv()
            s = scores(zz)
            m_old = mx_s[...]
            m_new = jnp.maximum(m_old, jnp.max(s, axis=-1, keepdims=True))
            e = jnp.exp(s - m_new)
            f = jnp.exp(m_old - m_new)
            mx_s[...] = m_new
            sum_s[...] = sum_s[...] * f + jnp.sum(e, axis=-1, keepdims=True)
            acc_s[...] = acc_s[...] * f + mm(e.astype(BF16), kv_all[1, zz].reshape(512, HEAD_DIM))

    phase('osend')
    o3 = (acc_s[...] / sum_s[...]).astype(BF16)
    for g in range(3):
        o_my[:, g * HEAD_DIM:(g + 1) * HEAD_DIM] = o3[g * R:(g + 1) * R]
    ocol = pl.ds(pl.multiple_of(x * GW, GW), GW)
    ocp = []
    for d in RING:
        rows = pl.ds(pl.multiple_of(lax.rem(x + d, 4) * T, T), T)
        c = rcopy(o_my.at[rows], o_cat.at[pl.ds(0, T), ocol], os_.at[d - 1], orr.at[d - 1], xp(d))
        c.start()
        ocp.append(c)
    o_cat[0:T, ocol] = o_my[myrows, :]
    out_k[...] = kx[...].astype(BF16)
    out_v[...] = vx[...].astype(BF16)

    phase('await')
    for i in range(2):
        acopy(i).wait_recv()
    cda.wait()

    def mcopy(i):
        b = pl.ds(groups[i][1], NG)
        return rcopy(m_my.at[:, b], m_oth.at[:, b], ds_.at[i], dr.at[i], mate)

    def down(i):
        ref, at = groups[i]
        cdw[i].wait()
        m_my[:, at:at + NG] = (mm(a_cat[:, LO:], ref[...])[0:T] + mm(a_cat[:, 0:LO], wda_s[:, at:at + NG])[0:T]).astype(BF16)
        mcopy(i).start()

    def pcopy(i):
        b = pl.ds(i * 1024, 1024)
        return rcopy(p_my.at[:, b], p_oth.at[:, b], ds_.at[6 + i], dr.at[6 + i], mate)

    phase('down0')
    for i in range(3):
        down(i)
    phase('down1')
    for i in range(3, 6):
        down(i)
    phase('owait')
    for c in ocp:
        c.wait_recv()
    for i in range(3):
        phase(f'wo{i}')
        co[i].wait()
        cols = slice(i * 1024, (i + 1) * 1024)
        p_my[:, cols] = mm(o_cat[...], woref[i][...])[0:T].astype(BF16)
        pcopy(i).start()
    phase('final')

    order = (3, 4, 5, 1, 2, 0)

    def final(i):
        cols = slice(groups[i][1], groups[i][1] + NG)
        mcopy(i).wait_recv()
        out_h[:, cols] = (hid_s[:, cols].astype(F32) + (p_my[:, cols].astype(F32) + p_oth[:, cols].astype(F32))
                          + (m_my[:, cols].astype(F32) + m_oth[:, cols].astype(F32))).astype(BF16)

    for i in range(3):
        pcopy(i).wait_recv()
        final(order[2 * i])
        final(order[2 * i + 1])

    phase('drain')
    for c in [hcp, fcp] + qcp + list(kcp.values()) + ocp + [mcopy(i) for i in range(6)] + [pcopy(i) for i in range(3)]:
        c.wait_send()
    for i in range(2):
        acopy(i).wait_send()
    for d in RING:
        when(k1_out[d], lambda d=d: k1(d).wait_send())
        when(v20_out[d], lambda d=d: v2(0, d).wait_send())

        for dy in range(4):
            when(z_out[d], lambda d=d, dy=dy: k2(dy, d).wait_send())
        when(z_out[d], lambda d=d: v1(d).wait_send())

        @pl.when(z_in[d])
        def _(d=d):
            for dy in RING:
                v2(d, dy).wait_send()
    phase(None)


def emit(h, k, v, out_h, out_k, out_v, sem):
    cps = [pltpu.make_async_copy(a, b, sem.at[i]) for i, (a, b) in enumerate(((h, out_h), (k, out_k), (v, out_v)))]
    for c in cps:
        c.start()
    for c in cps:
        c.wait()


def solution(mesh):
    inv = (1.0 / (np.float32(ROPE_BASE) ** (np.arange(0, HEAD_DIM, 2, dtype=np.float32) / np.float32(HEAD_DIM)))).astype(np.float32)
    inv = np.repeat(inv, 2).reshape(1, HEAD_DIM)

    def local_layer(hidden, positions, ln_gain, w_q, w_k, w_v, w_o, w_gate, w_up, w_down):
        vm = pl.BlockSpec(memory_space=pltpu.VMEM)
        hb = pl.BlockSpec(memory_space=pl.ANY)
        dma = pltpu.SemaphoreType.DMA
        V = pltpu.VMEM
        scratch = [
            V((T, D), BF16), V((1, T), jnp.int32), V((D // HEAD_DIM, HEAD_DIM), BF16), V((1, HEAD_DIM), F32),
            V((D, QW), BF16), V((D, KW), BF16), V((D, KW), BF16),
            V((D, FF), BF16), V((D, FF), BF16), V((LO, D), BF16), V((D, KW), BF16),
            V((R, D), BF16), V((T, QW), F32), V((T, KW), F32), V((T, KW), F32), V((R, HEAD_DIM), F32), V((R, HEAD_DIM), F32),
            V((4, T, GW), BF16), V((R, GW), BF16), V((4, 2, T, HEAD_DIM), BF16), V((2, 4, 4, R, HEAD_DIM), BF16),
            V((3 * R, 1), F32), V((3 * R, 1), F32), V((3 * R, HEAD_DIM), F32), V((R, GW), BF16), V((R, QW), BF16),
            V((T2, FF), BF16), V((R, FFT), BF16), V((T, D), BF16), V((T, D), BF16), V((T, D), BF16), V((T, D), BF16),
            dma((4,)), dma((26,)), dma((3,)), dma((3,)), dma((3,)), dma((3,)), dma((3,)), dma((3,)), dma((3,)), dma((3,)),
            dma((3,)), dma((3,)), dma((3,)), dma((3,)), dma((12,)), dma((12,)), dma((12,)), dma((12,)),
            dma((6,)), dma((6,)), dma((3,)), dma((3,)), dma((9,)), dma((9,)),
        ]
        outs = (jax.ShapeDtypeStruct((T, D), BF16), jax.ShapeDtypeStruct((R, HEAD_DIM), BF16), jax.ShapeDtypeStruct((R, HEAD_DIM), BF16))
        res = pl.pallas_call(
            kernel,
            name='layer',
            out_shape=tuple(pltpu.VMEM(o.shape, o.dtype) for o in outs),
            in_specs=[hb] * 11,
            out_specs=(vm, vm, vm),
            scratch_shapes=scratch,
            compiler_params=pltpu.CompilerParams(collective_id=0, has_side_effects=True, vmem_limit_bytes=60000000),
        )(hidden, positions.reshape(1, T), ln_gain.reshape(D // HEAD_DIM, HEAD_DIM), jnp.asarray(inv),
          w_q, w_k, w_v, w_o, w_gate, w_up, w_down)
        out_h, out_k, out_v = pl.pallas_call(
            emit,
            name='emit',
            out_shape=outs,
            in_specs=[vm] * 3,
            out_specs=(hb, hb, hb),
            scratch_shapes=[dma((3,))],
        )(*[pltpu.with_memory_space_constraint(r, pltpu.VMEM) for r in res])
        return out_h, out_k.reshape(T, 4, HEAD_DIM), out_v.reshape(T, 4, HEAD_DIM)

    row_spec = P(('dp', 'cp'), None)
    col_spec = P(None, 'tp')
    cache_spec = P(('dp', 'cp'), 'tp', None)
    in_specs = (row_spec, P(('dp', 'cp')), P(None), col_spec, col_spec, col_spec, P('tp', None), col_spec, col_spec, P('tp', None))
    return jax.shard_map(local_layer, mesh=mesh, in_specs=in_specs, out_specs=(row_spec, cache_spec, cache_spec), check_vma=False)
```

time: 35.9 us -> 32.9 us (0.916)
  Pallas kernels: 35.2 us -> 32 us
    pallas_call x1, Pallas kernels: 34.5 us -> 31.3 us  [local_layer(): pl.pallas_call(kernel, name='layer', out_shape=tuple((pltpu.VMEM(o.shape,...]
where the time goes in v2:
time: 32.9 us; the launch traced here: 32.8 us
  Pallas kernels  32 us (97%)
  between operations  0.8 us (2%)
    pallas_call x1, Pallas kernels, local_layer(): pl.pallas_call(kernel, name='layer', out_shape=tuple((pltpu.VMEM(o.shape,...  31.3 us
    pallas_call x1, Pallas kernels, local_layer(): pl.pallas_call(emit, name='emit', out_shape=outs, in_specs=[vm] * 3, out_...  0.72 us

profile of v2, /device:TPU:97, one launch (start us, length us, event | category | flops | bytes accessed | tf_op | source)
XLA Modules:
  0.0 32.8 jit_solution(7734365135910074657)
XLA Ops:
  0.6 31.3 %layer.1 = (bf16[32,3072]{1,0:T(8,128)(2,1)S(1)}, bf16[128,128]{1,0:T(8,128)(2,1)S(1)}, bf16[128,128]{1,0:T(8,128)(2,1)S(1)}) custom-call(bf16[32,3072]{1,0:T(8,128)(2,1)} %hid.1, s32[1,32]{1,0:T(1,128)} %bitcast.5, bf16[24,128]{1,0:T(8,128)(2,1)} %bitcast.4, f32[1,128]{1,0:T(1,128)} %constant.2.clone.invf, bf16[3072,1536]{1,0:T(8,128)(2,1)} %wq.1, ...), custom_call_target="tpu_custom_call" | custom-call | tf_op jit(solution)/shard_map/layer/pallas_call | solution.py:431
  31.9 0.7 %emit.1 = (bf16[32,3072]{1,0:T(8,128)(2,1)}, bf16[128,128]{1,0:T(8,128)(2,1)}, bf16[128,128]{1,0:T(8,128)(2,1)}) custom-call(bf16[32,3072]{1,0:T(8,128)(2,1)S(1)} %get-tuple-element.9.h, bf16[128,128]{1,0:T(8,128)(2,1)S(1)} %get-tuple-element.10.k, bf16[128,128]{1,0:T(8,128)(2,1)S(1)} %get-tuple-element.11.v), custom_call_target="tpu_custom_call" | custom-call | tf_op jit(solution)/shard_map/emit/pallas_call | solution.py:441

commit v3 on v2

--- a/solution.py
+++ b/solution.py
@@ -23,6 +23,7 @@
 KC = 4
 NG = 512
 NEG = -1e30
+SCALE = HEAD_DIM ** -0.5 * 1.4426950408889634
 F32 = jnp.float32
 BF16 = jnp.bfloat16
 RING = (1, 3, 2)
@@ -44,7 +45,7 @@
            wq_s, wk_s, wv_s, wg_s, wu_s, wda_s, wdx_s,
            h_all, accq, acck, accv, kx, vx, q_my, q_all, kv_my, kv_all,
            mx_s, sum_s, acc_s, o_my, o_cat,
-           a_my, a_cat, m_my, m_oth, p_my, p_oth,
+           a_my, a_cat, p_acc, m_my, m_oth, p_my, p_oth,
            i_sem, w_sem, hs, hr, fs, fr, qs, qr, ks, kr, k1s, k1r, v1s, v1r, k2s, k2r, v2s, v2r,
            as_, ar, os_, orr, ds_, dr):
     scope = []
@@ -103,6 +104,9 @@
         (wq_s.at[:, pl.ds(i * NG, NG)], i * NG) for i in range(3)]
     low = pl.ds(LO, D)
     cdw = [pltpu.make_async_copy(wd.at[low, pl.ds(at, NG)], ref, w_sem.at[20 + i]) for i, (ref, at) in enumerate(groups)]
+    for c in ckv:
+        c.start(priority=1)
+
     barrier = pltpu.get_barrier_semaphore()
     peers = [f(d) for f in (xp, yp, zp) for d in (1, 2, 3)] + [mate]
     for dev in peers:
@@ -124,8 +128,8 @@
     phase('ln')
     for c in small:
         c.wait()
-    for c in ckv + cwq + cgu + [cda, cdw[0]]:
-        c.start()
+    for c in cwq + cgu + [cda, cdw[0]]:
+        c.start(priority=1)
     hf = hid_s[...].astype(F32)
     mean = jnp.sum(hf, axis=-1, keepdims=True) * (1.0 / D)
     cen = hf - mean
@@ -186,7 +190,7 @@
         else:
             accq[...] += part
     for c in cdw[1:]:
-        c.start()
+        c.start(priority=1)
 
     def k1(d):
         b = kv_all.at[0, z, y]
@@ -272,7 +276,7 @@
                 v2(d, dy).start()
     gate_up(1)
     for c in co:
-        c.start()
+        c.start(priority=1)
 
     phase('qwait')
     for c in qcp:
@@ -281,7 +285,7 @@
 
     def scores(zz):
         kz = kv_all[0, zz].reshape(512, HEAD_DIM)
-        return lax.dot_general(q3, kz, (((1,), (1,)), ((), ())), preferred_element_type=F32) * (HEAD_DIM ** -0.5)
+        return lax.dot_general(q3, kz, (((1,), (1,)), ((), ())), preferred_element_type=F32)
 
     for d in RING:
         when(v20_in[d], lambda d=d: v2(0, d).wait_recv())
@@ -290,10 +294,35 @@
     col_tok = lax.broadcasted_iota(jnp.int32, (3 * R, 512), 1)
     s = jnp.where(col_tok <= row_tok, scores(z), NEG)
     m0 = jnp.max(s, axis=-1, keepdims=True)
-    e = jnp.exp(s - m0)
+    e = jnp.exp2((s - m0) * SCALE)
     mx_s[...] = m0
     sum_s[...] = jnp.sum(e, axis=-1, keepdims=True)
     acc_s[...] = mm(e.astype(BF16), kv_all[1, z].reshape(512, HEAD_DIM))
+
+    def mcopy(i):
+        b = pl.ds(groups[i][1], NG)
+        return rcopy(m_my.at[:, b], m_oth.at[:, b], ds_.at[i], dr.at[i], mate)
+
+    def down(i):
+        ref, at = groups[i]
+        cdw[i].wait()
+        m_my[:, at:at + NG] = (mm(a_cat[:, LO:], ref[...])[0:T] + mm(a_cat[:, 0:LO], wda_s[:, at:at + NG])[0:T]).astype(BF16)
+        mcopy(i).start()
+
+    def pcopy(i):
+        b = pl.ds(i * 1024, 1024)
+        return rcopy(p_my.at[:, b], p_oth.at[:, b], ds_.at[6 + i], dr.at[6 + i], mate)
+
+    def first_down():
+        for i in range(2):
+            acopy(i).wait_recv()
+        cda.wait()
+        for i in range(2):
+            down(i)
+
+    late = jnp.logical_and(jnp.logical_and(z == 3, y <= 1), x < 2)
+    phase('downB')
+    pl.when(late)(first_down)
 
     for dz in RING:
         phase(f'row{dz}')
@@ -308,8 +337,8 @@
             s = scores(zz)
             m_old = mx_s[...]
             m_new = jnp.maximum(m_old, jnp.max(s, axis=-1, keepdims=True))
-            e = jnp.exp(s - m_new)
-            f = jnp.exp(m_old - m_new)
+            e = jnp.exp2((s - m_new) * SCALE)
+            f = jnp.exp2((m_old - m_new) * SCALE)
             mx_s[...] = m_new
             sum_s[...] = sum_s[...] * f + jnp.sum(e, axis=-1, keepdims=True)
             acc_s[...] = acc_s[...] * f + mm(e.astype(BF16), kv_all[1, zz].reshape(512, HEAD_DIM))
@@ -329,40 +358,36 @@
     out_k[...] = kx[...].astype(BF16)
     out_v[...] = vx[...].astype(BF16)
 
-    phase('await')
-    for i in range(2):
-        acopy(i).wait_recv()
-    cda.wait()
-
-    def mcopy(i):
-        b = pl.ds(groups[i][1], NG)
-        return rcopy(m_my.at[:, b], m_oth.at[:, b], ds_.at[i], dr.at[i], mate)
-
-    def down(i):
-        ref, at = groups[i]
-        cdw[i].wait()
-        m_my[:, at:at + NG] = (mm(a_cat[:, LO:], ref[...])[0:T] + mm(a_cat[:, 0:LO], wda_s[:, at:at + NG])[0:T]).astype(BF16)
-        mcopy(i).start()
-
-    def pcopy(i):
-        b = pl.ds(i * 1024, 1024)
-        return rcopy(p_my.at[:, b], p_oth.at[:, b], ds_.at[6 + i], dr.at[6 + i], mate)
-
     phase('down0')
-    for i in range(3):
-        down(i)
+    pl.when(jnp.logical_not(late))(first_down)
+    down(2)
     phase('down1')
     for i in range(3, 6):
         down(i)
-    phase('owait')
-    for c in ocp:
-        c.wait_recv()
-    for i in range(3):
-        phase(f'wo{i}')
-        co[i].wait()
-        cols = slice(i * 1024, (i + 1) * 1024)
-        p_my[:, cols] = mm(o_cat[...], woref[i][...])[0:T].astype(BF16)
-        pcopy(i).start()
+    def wo_part(frm, first, last):
+        src = lax.rem(frm, 4)
+        cols = pl.ds(pl.multiple_of(src * GW, GW), GW)
+        rows = pl.ds(pl.multiple_of(src * GW, GW), GW)
+        for i in range(3):
+            pcols = slice(i * 1024, (i + 1) * 1024)
+            part = mm(o_cat[:, cols], woref[i][rows, :])[0:T]
+            if not first:
+                part = p_acc[:, pcols] + part
+            if last:
+                p_my[:, pcols] = part.astype(BF16)
+                pcopy(i).start()
+            else:
+                p_acc[:, pcols] = part
+
+    phase('woown')
+    for c in co:
+        c.wait()
+    wo_part(x, True, False)
+    for n, d in enumerate(RING):
+        phase(f'owait{d}')
+        ocp[n].wait_recv()
+        phase(f'wo{d}')
+        wo_part(x + 4 - d, False, n == 2)
     phase('final')
 
     order = (3, 4, 5, 1, 2, 0)
@@ -422,7 +447,7 @@
             V((R, D), BF16), V((T, QW), F32), V((T, KW), F32), V((T, KW), F32), V((R, HEAD_DIM), F32), V((R, HEAD_DIM), F32),
             V((4, T, GW), BF16), V((R, GW), BF16), V((4, 2, T, HEAD_DIM), BF16), V((2, 4, 4, R, HEAD_DIM), BF16),
             V((3 * R, 1), F32), V((3 * R, 1), F32), V((3 * R, HEAD_DIM), F32), V((R, GW), BF16), V((R, QW), BF16),
-            V((T2, FF), BF16), V((R, FFT), BF16), V((T, D), BF16), V((T, D), BF16), V((T, D), BF16), V((T, D), BF16),
+            V((T2, FF), BF16), V((R, FFT), BF16), V((T, D), F32), V((T, D), BF16), V((T, D), BF16), V((T, D), BF16), V((T, D), BF16),
             dma((4,)), dma((26,)), dma((3,)), dma((3,)), dma((3,)), dma((3,)), dma((3,)), dma((3,)), dma((3,)), dma((3,)),
             dma((3,)), dma((3,)), dma((3,)), dma((3,)), dma((12,)), dma((12,)), dma((12,)), dma((12,)),
             dma((6,)), dma((6,)), dma((3,)), dma((3,)), dma((9,)), dma((9,)),

time: 32.9 us -> 32.2 us (0.979)
  Pallas kernels: 32 us -> 31.3 us
    pallas_call x1, Pallas kernels: 31.3 us -> 30.6 us  [local_layer(): pl.pallas_call(kernel, name='layer', out_shape=tuple((pltpu.VMEM(o.shape,...]
where the time goes in v3:
time: 32.2 us; the launch traced here: 32.1 us
  Pallas kernels  31.3 us (97%)
  between operations  0.8 us (2%)
    pallas_call x1, Pallas kernels, local_layer(): pl.pallas_call(kernel, name='layer', out_shape=tuple((pltpu.VMEM(o.shape,...  30.6 us
    pallas_call x1, Pallas kernels, local_layer(): pl.pallas_call(emit, name='emit', out_shape=outs, in_specs=[vm] * 3, out_...  0.72 us

profile of v3, /device:TPU:97, one launch (start us, length us, event | category | flops | bytes accessed | tf_op | source)
XLA Modules:
  0.0 32.1 jit_solution(9829142824484507781)
XLA Ops:
  0.6 30.6 %layer.1 = (bf16[32,3072]{1,0:T(8,128)(2,1)S(1)}, bf16[128,128]{1,0:T(8,128)(2,1)S(1)}, bf16[128,128]{1,0:T(8,128)(2,1)S(1)}) custom-call(bf16[32,3072]{1,0:T(8,128)(2,1)} %hid.1, s32[1,32]{1,0:T(1,128)} %bitcast.5, bf16[24,128]{1,0:T(8,128)(2,1)} %bitcast.4, f32[1,128]{1,0:T(1,128)} %constant.2.clone.invf, bf16[3072,1536]{1,0:T(8,128)(2,1)} %wq.1, ...), custom_call_target="tpu_custom_call" | custom-call | tf_op jit(solution)/shard_map/layer/pallas_call | solution.py:456
  31.2 0.7 %emit.1 = (bf16[32,3072]{1,0:T(8,128)(2,1)}, bf16[128,128]{1,0:T(8,128)(2,1)}, bf16[128,128]{1,0:T(8,128)(2,1)}) custom-call(bf16[32,3072]{1,0:T(8,128)(2,1)S(1)} %get-tuple-element.9.h, bf16[128,128]{1,0:T(8,128)(2,1)S(1)} %get-tuple-element.10.k, bf16[128,128]{1,0:T(8,128)(2,1)S(1)} %get-tuple-element.11.v), custom_call_target="tpu_custom_call" | custom-call | tf_op jit(solution)/shard_map/emit/pallas_call | solution.py:466

commit v4 on v3

--- a/solution.py
+++ b/solution.py
@@ -20,7 +20,8 @@
 FC = 1024
 LO = 1024
 FFT = 4096
-KC = 4
+KC = 2
+Q2 = 768
 NG = 512
 NEG = -1e30
 SCALE = HEAD_DIM ** -0.5 * 1.4426950408889634
@@ -43,10 +44,10 @@
            out_h, out_k, out_v,
            hid_s, pos_s, gain_s, inv_s,
            wq_s, wk_s, wv_s, wg_s, wu_s, wda_s, wdx_s,
-           h_all, accq, acck, accv, kx, vx, q_my, q_all, kv_my, kv_all,
+           h_all, cs_s, accq, acck, accv, kx, vx, q_my, q_all, kv_my, kv_all,
            mx_s, sum_s, acc_s, o_my, o_cat,
-           a_my, a_cat, p_acc, m_my, m_oth, p_my, p_oth,
-           i_sem, w_sem, hs, hr, fs, fr, qs, qr, ks, kr, k1s, k1r, v1s, v1r, k2s, k2r, v2s, v2r,
+           a_my, a_cat, m_my, m_oth, p_my, p_oth,
+           i_sem, w_sem, cs_sem, hs, hr, fs, fr, qs, qr, ks, kr, k1s, k1r, v1s, v1r, k2s, k2r, v2s, v2r,
            as_, ar, os_, orr, ds_, dr):
     scope = []
 
@@ -74,6 +75,9 @@
         return tp, lax.rem(z + d, 4) * 16 + y * 4 + x
 
     mate = (1 - tp, cp)
+
+    def when(cond, fn):
+        pl.when(cond)(lambda: fn())
 
     def rcopy(src, dst, ss, rs, dev):
         return pltpu.make_async_remote_copy(
@@ -88,9 +92,10 @@
     ckv = [pltpu.make_async_copy(src.at[pl.ds(i * half, half)], dst.at[pl.ds(i * half, half)], w_sem.at[2 * i + n])
            for i in range(2) for n, (src, dst) in enumerate(((wk, wk_s), (wv, wv_s)))]
     kc = D // KC
-    cwq = [pltpu.make_async_copy(wq.at[pl.ds(i * kc, kc)], wq_s.at[pl.ds(i * kc, kc)], w_sem.at[4 + i]) for i in range(KC)]
     par = lax.rem(x, 2)
     pair = (tp, cp + 1 - 2 * par)
+    qcol = pl.ds(pl.multiple_of(par * Q2, Q2), Q2)
+    cwq = [pltpu.make_async_copy(wq.at[pl.ds(i * kc, kc), qcol], wq_s.at[pl.ds(i * kc, kc), pl.ds(0, Q2)], w_sem.at[4 + i]) for i in range(KC)]
     mine = pl.ds(pl.multiple_of(par * T, T), T)
     theirs = pl.ds(pl.multiple_of((1 - par) * T, T), T)
     hcol = pl.ds(pl.multiple_of(tp * QW, QW), QW)
@@ -152,6 +157,9 @@
     cos = jnp.cos(ang)
     sin = jnp.sin(ang)
     even = lax.rem(lax.broadcasted_iota(jnp.int32, (T, HEAD_DIM), 1), 2) == 0
+    cs_s[0, mine] = cos
+    cs_s[1, mine] = sin
+    cscp = rcopy(cs_s.at[:, mine], cs_s.at[:, mine], cs_sem.at[0], cs_sem.at[1], pair)
 
     phase('kvproj')
     for i in range(2):
@@ -179,17 +187,9 @@
     for d in RING:
         kcp[d].start()
     hcp.start()
-
-    phase('qproj')
-    for i in range(KC):
-        rows = slice(i * kc, (i + 1) * kc)
-        cwq[i].wait()
-        part = mm(h_all[mine, rows], wq_s[rows, :])
-        if i == 0:
-            accq[...] = part
-        else:
-            accq[...] += part
-    for c in cdw[1:]:
+    cscp.start()
+
+    for c in cdw[1:3]:
         c.start(priority=1)
 
     def k1(d):
@@ -215,9 +215,6 @@
     v20_out = {d: y + d <= 3 for d in RING}
     v20_in = {d: y >= d for d in RING}
 
-    def when(cond, fn):
-        pl.when(cond)(lambda: fn())
-
     phase('kvx')
     for d in RING:
         kcp[d].wait_recv()
@@ -233,25 +230,59 @@
     hcp.wait_recv()
     fcp.start()
 
-    phase('qrope')
-    for j in range(12):
-        cols = slice(j * HEAD_DIM, (j + 1) * HEAD_DIM)
-        q_my[j // 3, :, (j % 3) * HEAD_DIM:(j % 3 + 1) * HEAD_DIM] = rope(
-            accq[:, cols].astype(BF16).astype(F32), cos, sin, even)
-    qcp = []
-    for d in RING:
-        dst = lax.rem(x + d, 4)
-        c = rcopy(q_my.at[dst], q_all.at[myrows], qs.at[d - 1], qr.at[d - 1], xp(d))
-        c.start()
-        qcp.append(c)
-    q_all[myrows, :] = q_my[x]
-
     def acopy(i):
         cols = pl.ds(pl.multiple_of(par * FF + i * FC, FC), FC)
         return rcopy(a_my.at[theirs, pl.ds(i * FC, FC)], a_cat.at[pl.ds(0, T), cols], as_.at[i], ar.at[i], pair)
 
+    def pass_on():
+        for d in RING:
+            when(k1_in[d], lambda d=d: k1(d).wait_recv())
+            for dz in RING:
+                when(z_out[dz], lambda d=d, dz=dz: k2(d, dz).start())
+
+            @pl.when(z_in[d])
+            def _(d=d):
+                v1(d).wait_recv()
+                for dy in RING:
+                    v2(d, dy).start()
+
+    soon = jnp.logical_and(tp == 1, y >= 1)
+    next_ = jnp.logical_and(tp == 0, y >= 2)
+    last = jnp.logical_and(tp == 0, jnp.logical_and(y == 0, z < 3))
+    third = jnp.logical_not(jnp.logical_or(last, jnp.logical_or(soon, next_)))
+
+    phase('k1a')
+    pl.when(soon)(pass_on)
     phase('fwait')
     fcp.wait_recv()
+
+    phase('qproj')
+    for c in cwq:
+        c.wait()
+    accq[...] = mm(h_all[...], wq_s[:, 0:Q2])[0:T2]
+    for c in cdw[3:]:
+        c.start(priority=1)
+    phase('qrope')
+    cscp.wait_recv()
+    even2 = lax.rem(lax.broadcasted_iota(jnp.int32, (T2, HEAD_DIM), 1), 2) == 0
+    for j in range(6):
+        cols = slice(j * HEAD_DIM, (j + 1) * HEAD_DIM)
+        q_my[j // 3, :, (j % 3) * HEAD_DIM:(j % 3 + 1) * HEAD_DIM] = rope(
+            accq[:, cols].astype(BF16).astype(F32), cs_s[0], cs_s[1], even2)
+    prow = pl.ds(pl.multiple_of((x // 2) * T2, T2), T2)
+
+    def qcopy(n):
+        return rcopy(q_my.at[n], q_all.at[prow], qs.at[n], qr.at[x // 2], (tp, cp - x + 2 * par + n))
+
+    def qlocal(n):
+        q_all[prow, :] = q_my[n]
+
+    def qarrive(i):
+        rcopy(q_my.at[0], q_all.at[pl.ds(i * T2, T2)], qs.at[0], qr.at[i], pair).wait_recv()
+
+    for n in range(2):
+        when(2 * par + n != x, lambda n=n: qcopy(n).start())
+        when(2 * par + n == x, lambda n=n: qlocal(n))
     def gate_up(i):
         phase(f'gu{i}')
         cols = slice(i * FC, (i + 1) * FC)
@@ -262,25 +293,20 @@
         a_my[:, cols] = (g * jax.nn.sigmoid(g) * u).astype(BF16)
         acopy(i).start()
         a_cat[0:T, pl.ds(pl.multiple_of(par * FF + i * FC, FC), FC)] = a_my[mine, cols]
+    phase('k1b')
+    pl.when(next_)(pass_on)
     gate_up(0)
-    phase('k1wait')
-    for d in RING:
-        when(k1_in[d], lambda d=d: k1(d).wait_recv())
-        for dz in RING:
-            when(z_out[dz], lambda d=d, dz=dz: k2(d, dz).start())
-
-        @pl.when(z_in[d])
-        def _(d=d):
-            v1(d).wait_recv()
-            for dy in RING:
-                v2(d, dy).start()
+    phase('k1c')
+    pl.when(third)(pass_on)
     gate_up(1)
+    phase('k1d')
+    pl.when(last)(pass_on)
     for c in co:
         c.start(priority=1)
 
     phase('qwait')
-    for c in qcp:
-        c.wait_recv()
+    for i in range(2):
+        when(2 * i + x // 2 != x, lambda i=i: qarrive(i))
     q3 = jnp.concatenate([q_all[:, g * HEAD_DIM:(g + 1) * HEAD_DIM] for g in range(3)], axis=0)
 
     def scores(zz):
@@ -319,10 +345,6 @@
         cda.wait()
         for i in range(2):
             down(i)
-
-    late = jnp.logical_and(jnp.logical_and(z == 3, y <= 1), x < 2)
-    phase('downB')
-    pl.when(late)(first_down)
 
     for dz in RING:
         phase(f'row{dz}')
@@ -359,35 +381,20 @@
     out_v[...] = vx[...].astype(BF16)
 
     phase('down0')
-    pl.when(jnp.logical_not(late))(first_down)
+    first_down()
     down(2)
     phase('down1')
     for i in range(3, 6):
         down(i)
-    def wo_part(frm, first, last):
-        src = lax.rem(frm, 4)
-        cols = pl.ds(pl.multiple_of(src * GW, GW), GW)
-        rows = pl.ds(pl.multiple_of(src * GW, GW), GW)
-        for i in range(3):
-            pcols = slice(i * 1024, (i + 1) * 1024)
-            part = mm(o_cat[:, cols], woref[i][rows, :])[0:T]
-            if not first:
-                part = p_acc[:, pcols] + part
-            if last:
-                p_my[:, pcols] = part.astype(BF16)
-                pcopy(i).start()
-            else:
-                p_acc[:, pcols] = part
-
-    phase('woown')
-    for c in co:
-        c.wait()
-    wo_part(x, True, False)
-    for n, d in enumerate(RING):
-        phase(f'owait{d}')
-        ocp[n].wait_recv()
-        phase(f'wo{d}')
-        wo_part(x + 4 - d, False, n == 2)
+    phase('owait')
+    for c in ocp:
+        c.wait_recv()
+    for i in range(3):
+        phase(f'wo{i}')
+        pcols = slice(i * 1024, (i + 1) * 1024)
+        co[i].wait()
+        p_my[:, pcols] = mm(o_cat[...], woref[i][...])[0:T].astype(BF16)
+        pcopy(i).start()
     phase('final')
 
     order = (3, 4, 5, 1, 2, 0)
@@ -404,7 +411,9 @@
         final(order[2 * i + 1])
 
     phase('drain')
-    for c in [hcp, fcp] + qcp + list(kcp.values()) + ocp + [mcopy(i) for i in range(6)] + [pcopy(i) for i in range(3)]:
+    for n in range(2):
+        when(2 * par + n != x, lambda n=n: qcopy(n).wait_send())
+    for c in [hcp, fcp, cscp] + list(kcp.values()) + ocp + [mcopy(i) for i in range(6)] + [pcopy(i) for i in range(3)]:
         c.wait_send()
     for i in range(2):
         acopy(i).wait_send()
@@ -444,11 +453,11 @@
             V((T, D), BF16), V((1, T), jnp.int32), V((D // HEAD_DIM, HEAD_DIM), BF16), V((1, HEAD_DIM), F32),
             V((D, QW), BF16), V((D, KW), BF16), V((D, KW), BF16),
             V((D, FF), BF16), V((D, FF), BF16), V((LO, D), BF16), V((D, KW), BF16),
-            V((R, D), BF16), V((T, QW), F32), V((T, KW), F32), V((T, KW), F32), V((R, HEAD_DIM), F32), V((R, HEAD_DIM), F32),
-            V((4, T, GW), BF16), V((R, GW), BF16), V((4, 2, T, HEAD_DIM), BF16), V((2, 4, 4, R, HEAD_DIM), BF16),
+            V((R, D), BF16), V((2, T2, HEAD_DIM), F32), V((T2, Q2), F32), V((T, KW), F32), V((T, KW), F32), V((R, HEAD_DIM), F32), V((R, HEAD_DIM), F32),
+            V((2, T2, GW), BF16), V((R, GW), BF16), V((4, 2, T, HEAD_DIM), BF16), V((2, 4, 4, R, HEAD_DIM), BF16),
             V((3 * R, 1), F32), V((3 * R, 1), F32), V((3 * R, HEAD_DIM), F32), V((R, GW), BF16), V((R, QW), BF16),
-            V((T2, FF), BF16), V((R, FFT), BF16), V((T, D), F32), V((T, D), BF16), V((T, D), BF16), V((T, D), BF16), V((T, D), BF16),
-            dma((4,)), dma((26,)), dma((3,)), dma((3,)), dma((3,)), dma((3,)), dma((3,)), dma((3,)), dma((3,)), dma((3,)),
+            V((T2, FF), BF16), V((R, FFT), BF16), V((T, D), BF16), V((T, D), BF16), V((T, D), BF16), V((T, D), BF16),
+            dma((4,)), dma((26,)), dma((2,)), dma((3,)), dma((3,)), dma((3,)), dma((3,)), dma((3,)), dma((3,)), dma((3,)), dma((3,)),
             dma((3,)), dma((3,)), dma((3,)), dma((3,)), dma((12,)), dma((12,)), dma((12,)), dma((12,)),
             dma((6,)), dma((6,)), dma((3,)), dma((3,)), dma((9,)), dma((9,)),
         ]

time: 32.2 us -> 31.1 us (0.966)
  Pallas kernels: 31.3 us -> 30.1 us
    pallas_call x1, Pallas kernels: 30.6 us -> 29.4 us  [local_layer(): pl.pallas_call(kernel, name='layer', out_shape=tuple((pltpu.VMEM(o.shape,...]
where the time goes in v4:
time: 31.1 us; the launch traced here: 30.9 us
  Pallas kernels  30.1 us (97%)
  between operations  0.8 us (3%)
    pallas_call x1, Pallas kernels, local_layer(): pl.pallas_call(kernel, name='layer', out_shape=tuple((pltpu.VMEM(o.shape,...  29.4 us
    pallas_call x1, Pallas kernels, local_layer(): pl.pallas_call(emit, name='emit', out_shape=outs, in_specs=[vm] * 3, out_...  0.72 us

profile of v4, /device:TPU:97, one launch (start us, length us, event | category | flops | bytes accessed | tf_op | source)
XLA Modules:
  0.0 30.9 jit_solution(5909353228958675135)
XLA Ops:
  0.6 29.4 %layer.1 = (bf16[32,3072]{1,0:T(8,128)(2,1)S(1)}, bf16[128,128]{1,0:T(8,128)(2,1)S(1)}, bf16[128,128]{1,0:T(8,128)(2,1)S(1)}) custom-call(bf16[32,3072]{1,0:T(8,128)(2,1)} %hid.1, s32[1,32]{1,0:T(1,128)} %bitcast.5, bf16[24,128]{1,0:T(8,128)(2,1)} %bitcast.4, f32[1,128]{1,0:T(1,128)} %constant.2.clone.invf, bf16[3072,1536]{1,0:T(8,128)(2,1)} %wq.1, ...), custom_call_target="tpu_custom_call" | custom-call | tf_op jit(solution)/shard_map/layer/pallas_call | solution.py:465
  30.1 0.7 %emit.1 = (bf16[32,3072]{1,0:T(8,128)(2,1)}, bf16[128,128]{1,0:T(8,128)(2,1)}, bf16[128,128]{1,0:T(8,128)(2,1)}) custom-call(bf16[32,3072]{1,0:T(8,128)(2,1)S(1)} %get-tuple-element.9.h, bf16[128,128]{1,0:T(8,128)(2,1)S(1)} %get-tuple-element.10.k, bf16[128,128]{1,0:T(8,128)(2,1)S(1)} %get-tuple-element.11.v), custom_call_target="tpu_custom_call" | custom-call | tf_op jit(solution)/shard_map/emit/pallas_call | solution.py:475

commit v5 on v4

--- a/solution.py
+++ b/solution.py
@@ -105,10 +105,11 @@
     cda = pltpu.make_async_copy(wd.at[pl.ds(0, LO)], wda_s, w_sem.at[16])
     woref = [wg_s.at[pl.ds(0, QW), pl.ds(0, 1024)], wg_s.at[pl.ds(0, QW), pl.ds(1024, 1024)], wg_s.at[pl.ds(QW, QW), pl.ds(0, 1024)]]
     co = [pltpu.make_async_copy(wo.at[:, pl.ds(i * 1024, 1024)], woref[i], w_sem.at[17 + i]) for i in range(3)]
-    groups = [(wdx_s.at[:], 5 * NG), (wk_s.at[:], 3 * NG), (wv_s.at[:], 4 * NG)] + [
+    pieces = [(wdx_s.at[:], 5 * NG), (wk_s.at[:], 3 * NG), (wv_s.at[:], 4 * NG)] + [
         (wq_s.at[:, pl.ds(i * NG, NG)], i * NG) for i in range(3)]
+    groups = [(wdx_s, 5 * NG, NG), (wk_s, 3 * NG, NG), (wv_s, 4 * NG, NG), (wq_s, 0, 3 * NG)]
     low = pl.ds(LO, D)
-    cdw = [pltpu.make_async_copy(wd.at[low, pl.ds(at, NG)], ref, w_sem.at[20 + i]) for i, (ref, at) in enumerate(groups)]
+    cdw = [pltpu.make_async_copy(wd.at[low, pl.ds(at, NG)], ref, w_sem.at[20 + i]) for i, (ref, at) in enumerate(pieces)]
     for c in ckv:
         c.start(priority=1)
 
@@ -248,7 +249,7 @@
 
     soon = jnp.logical_and(tp == 1, y >= 1)
     next_ = jnp.logical_and(tp == 0, y >= 2)
-    last = jnp.logical_and(tp == 0, jnp.logical_and(y == 0, z < 3))
+    last = jnp.logical_and(tp == 0, jnp.logical_and(y == 0, z == 0))
     third = jnp.logical_not(jnp.logical_or(last, jnp.logical_or(soon, next_)))
 
     phase('k1a')
@@ -326,17 +327,18 @@
     acc_s[...] = mm(e.astype(BF16), kv_all[1, z].reshape(512, HEAD_DIM))
 
     def mcopy(i):
-        b = pl.ds(groups[i][1], NG)
+        b = pl.ds(groups[i][1], groups[i][2])
         return rcopy(m_my.at[:, b], m_oth.at[:, b], ds_.at[i], dr.at[i], mate)
 
     def down(i):
-        ref, at = groups[i]
-        cdw[i].wait()
-        m_my[:, at:at + NG] = (mm(a_cat[:, LO:], ref[...])[0:T] + mm(a_cat[:, 0:LO], wda_s[:, at:at + NG])[0:T]).astype(BF16)
+        ref, at, n = groups[i]
+        for c in cdw[i:i + n // NG]:
+            c.wait()
+        m_my[:, at:at + n] = (mm(a_cat[:, LO:], ref[...])[0:T] + mm(a_cat[:, 0:LO], wda_s[:, at:at + n])[0:T]).astype(BF16)
         mcopy(i).start()
 
     def pcopy(i):
-        b = pl.ds(i * 1024, 1024)
+        b = pl.ds(2048 * i, 2048 - 1024 * i)
         return rcopy(p_my.at[:, b], p_oth.at[:, b], ds_.at[6 + i], dr.at[6 + i], mate)
 
     def first_down():
@@ -384,36 +386,36 @@
     first_down()
     down(2)
     phase('down1')
-    for i in range(3, 6):
-        down(i)
+    down(3)
     phase('owait')
     for c in ocp:
         c.wait_recv()
-    for i in range(3):
-        phase(f'wo{i}')
-        pcols = slice(i * 1024, (i + 1) * 1024)
-        co[i].wait()
-        p_my[:, pcols] = mm(o_cat[...], woref[i][...])[0:T].astype(BF16)
-        pcopy(i).start()
+    co[0].wait()
+    co[1].wait()
+    phase('wo0')
+    p_my[:, 0:2048] = mm(o_cat[...], wg_s[0:QW, :])[0:T].astype(BF16)
+    pcopy(0).start()
+    co[2].wait()
+    phase('wo1')
+    p_my[:, 2048:D] = mm(o_cat[...], wg_s[QW:D, 0:1024])[0:T].astype(BF16)
+    pcopy(1).start()
     phase('final')
 
-    order = (3, 4, 5, 1, 2, 0)
-
-    def final(i):
-        cols = slice(groups[i][1], groups[i][1] + NG)
-        mcopy(i).wait_recv()
+    def final(cols):
         out_h[:, cols] = (hid_s[:, cols].astype(F32) + (p_my[:, cols].astype(F32) + p_oth[:, cols].astype(F32))
                           + (m_my[:, cols].astype(F32) + m_oth[:, cols].astype(F32))).astype(BF16)
 
-    for i in range(3):
-        pcopy(i).wait_recv()
-        final(order[2 * i])
-        final(order[2 * i + 1])
+    for i in range(4):
+        mcopy(i).wait_recv()
+    pcopy(0).wait_recv()
+    final(slice(0, 2048))
+    pcopy(1).wait_recv()
+    final(slice(2048, D))
 
     phase('drain')
     for n in range(2):
         when(2 * par + n != x, lambda n=n: qcopy(n).wait_send())
-    for c in [hcp, fcp, cscp] + list(kcp.values()) + ocp + [mcopy(i) for i in range(6)] + [pcopy(i) for i in range(3)]:
+    for c in [hcp, fcp, cscp] + list(kcp.values()) + ocp + [mcopy(i) for i in range(4)] + [pcopy(i) for i in range(2)]:
         c.wait_send()
     for i in range(2):
         acopy(i).wait_send()

time: 31.1 us -> 30.9 us (level)
  no operation moved by 1% of the time
where the time goes in v5:
time: 30.9 us; the launch traced here: 30.8 us
  Pallas kernels  30 us (97%)
  between operations  0.8 us (3%)
    pallas_call x1, Pallas kernels, local_layer(): pl.pallas_call(kernel, name='layer', out_shape=tuple((pltpu.VMEM(o.shape,...  29.2 us
    pallas_call x1, Pallas kernels, local_layer(): pl.pallas_call(emit, name='emit', out_shape=outs, in_specs=[vm] * 3, out_...  0.72 us

profile of v5, /device:TPU:97, one launch (start us, length us, event | category | flops | bytes accessed | tf_op | source)
XLA Modules:
  0.0 30.8 jit_solution(13125139894352749497)
XLA Ops:
  0.6 29.2 %layer.1 = (bf16[32,3072]{1,0:T(8,128)(2,1)S(1)}, bf16[128,128]{1,0:T(8,128)(2,1)S(1)}, bf16[128,128]{1,0:T(8,128)(2,1)S(1)}) custom-call(bf16[32,3072]{1,0:T(8,128)(2,1)} %hid.1, s32[1,32]{1,0:T(1,128)} %bitcast.5, bf16[24,128]{1,0:T(8,128)(2,1)} %bitcast.4, f32[1,128]{1,0:T(1,128)} %constant.2.clone.invf, bf16[3072,1536]{1,0:T(8,128)(2,1)} %wq.1, ...), custom_call_target="tpu_custom_call" | custom-call | tf_op jit(solution)/shard_map/layer/pallas_call | solution.py:467
  29.9 0.7 %emit.1 = (bf16[32,3072]{1,0:T(8,128)(2,1)}, bf16[128,128]{1,0:T(8,128)(2,1)}, bf16[128,128]{1,0:T(8,128)(2,1)}) custom-call(bf16[32,3072]{1,0:T(8,128)(2,1)S(1)} %get-tuple-element.9.h, bf16[128,128]{1,0:T(8,128)(2,1)S(1)} %get-tuple-element.10.k, bf16[128,128]{1,0:T(8,128)(2,1)S(1)} %get-tuple-element.11.v), custom_call_target="tpu_custom_call" | custom-call | tf_op jit(solution)/shard_map/emit/pallas_call | solution.py:477
